TPU v7x, 32 devices: a whole 2x2x4 slice. The times are simulated.
32 devices in a mesh: fsdp: 32 (over z, y, x, core).
Axes of the slice: x: 2, y: 2, z: 4, core: 2. Of those that a mesh axis runs over, the one named last changes fastest.
Arguments:
- tokens: bfloat16 [32768, 768], P('fsdp'), may hold values from -80 to 80
- segment_ids: int32 [32768], P('fsdp'), may hold values from 0 to 20, as said below
- pad_mask: int32 [32768], P('fsdp'), may hold values from 0 to 1, as said below
- w_qkv: bfloat16 [768, 2304], P('fsdp'), may hold values from -0.25 to 0.25
- bias_query: bfloat16 [768], P('fsdp'), may hold values from -3 to 3
- bias_value: bfloat16 [768], P('fsdp'), may hold values from -3 to 3
- w_out: bfloat16 [768, 768], P('fsdp'), may hold values from -1.25 to 1.25
- bias_out: bfloat16 [768], P('fsdp'), may hold values from -3 to 3
- gain_one: bfloat16 [768], P('fsdp'), may hold values from 0.25 to 1.75
- shift_one: bfloat16 [768], P('fsdp'), may hold values from -3 to 3
- w_up: bfloat16 [768, 3072], P('fsdp'), may hold values from -0.21875 to 0.21875
- bias_up: bfloat16 [3072], P('fsdp'), may hold values from -3 to 3
- w_down: bfloat16 [3072, 768], P('fsdp'), may hold values from -0.109375 to 0.109375
- bias_down: bfloat16 [768], P('fsdp'), may hold values from -3 to 3
- gain_two: bfloat16 [768], P('fsdp'), may hold values from 0.25 to 1.75
- shift_two: bfloat16 [768], P('fsdp'), may hold values from -3 to 3
- cotangent: bfloat16 [32768, 768], P('fsdp'), may hold values from -6 to 6
Outputs:
- layer_out: bfloat16 [32768, 768], P('fsdp')
- grad_tokens: float32 [32768, 768], P('fsdp')
- grad_w_qkv: float32 [768, 2304], P('fsdp')
- grad_bias_query: float32 [768], P('fsdp')
- grad_bias_value: float32 [768], P('fsdp')
- grad_w_out: float32 [768, 768], P('fsdp')
- grad_bias_out: float32 [768], P('fsdp')
- grad_gain_one: float32 [768], P('fsdp')
- grad_shift_one: float32 [768], P('fsdp')
- grad_w_up: float32 [768, 3072], P('fsdp')
- grad_bias_up: float32 [3072], P('fsdp')
- grad_w_down: float32 [3072, 768], P('fsdp')
- grad_bias_down: float32 [768], P('fsdp')
- grad_gain_two: float32 [768], P('fsdp')
- grad_shift_two: float32 [768], P('fsdp')
Inputs may be any that keep to these rules, and one draw needn't show every extreme that they name: `segment_ids`: sequence numbers of the packed tokens, starting at 0 and never falling; there are exactly 21 sequences, each of 1024 to 2048 tokens, and one holds exactly 2048. `pad_mask`: the first token of every sequence is 1.
All inputs are finite; a program needn't handle non-finite values.
Results may differ from a plain program's by a relative error of at most 0.015.
The roundings to bfloat16 on the way count: a program that leaves them out, or rounds other values in their place, can miss the bound.
Values may be sent and summed in bfloat16 or wider, within the bound.
A program may use at most 320 MiB of HBM per device.

v0:
```python
import functools

import jax
import jax.numpy as jnp
from jax import lax
from jax.experimental import pallas as pl
from jax.experimental.pallas import tpu as pltpu
from jax.sharding import PartitionSpec as P

D = 768
HEADS = 12
HEAD_DIM = 64
LEN_MAX = 2048
GROUP = 4
OWN_HEADS = HEADS // GROUP
Q_ROWS = OWN_HEADS * HEAD_DIM
KV_ROWS = 2 * Q_ROWS
MIX_ROWS = Q_ROWS + KV_ROWS
BQ = 512
FK = 512
BK = 256
NEG = -1e30

bf16 = jnp.bfloat16
f32 = jnp.float32
eps_norm = 1e-12
score_scale = 0.125

NN = (((1,), (0,)), ((), ()))
NT = (((1,), (1,)), ((), ()))


def mm(a, b, dims=NN):
    return lax.dot_general(a, b, dims, preferred_element_type=f32)


def norm_rows(hidden, gain_row, shift_row):
    centre = hidden - jnp.mean(hidden, axis=-1, keepdims=True)
    spread = jnp.mean(centre * centre, axis=-1, keepdims=True)
    return centre * lax.rsqrt(spread + eps_norm) * gain_row + shift_row


def gelu_exact(pre_act):
    return 0.5 * pre_act * (1.0 + jax.scipy.special.erf(pre_act * 0.7071067811865476))


def head_rows(block, h, upper):
    zero = jnp.zeros_like(block[:HEAD_DIM])
    rows = block[h * HEAD_DIM : (h + 1) * HEAD_DIM]
    return jnp.concatenate([zero, rows] if upper else [rows, zero], axis=0)


def attend_kernel(
    span, qtag_ref, ktag_ref, qt_ref, kv_ref, kvt_ref, ot_ref, lse_ref, m_sc, l_sc, acc_sc
):
    i = pl.program_id(0)
    m_sc[...] = jnp.full_like(m_sc, NEG)
    l_sc[...] = jnp.zeros_like(l_sc)
    acc_sc[...] = jnp.zeros_like(acc_sc)
    qtag = qtag_ref[...]
    qt = qt_ref[...]
    q_pad = [head_rows(qt, h, False) for h in range(OWN_HEADS)]

    def step(kb, carry):
        rows = pl.ds(pl.multiple_of(kb * FK, FK), FK)
        seen = ktag_ref[rows, :] == qtag
        hs = range(OWN_HEADS)
        s = [mm(kv_ref[rows, 128 * h : 128 * (h + 1)], q_pad[h]) for h in hs]
        s = [jnp.where(seen, v, NEG) for v in s]
        m_old = [m_sc[h : h + 1, :] for h in hs]
        l_old = [l_sc[h : h + 1, :] for h in hs]
        m_new = [jnp.maximum(m_old[h], jnp.max(s[h], axis=0, keepdims=True)) for h in hs]
        p = [jnp.exp(s[h] - m_new[h]).astype(bf16) for h in hs]
        fade = [jnp.exp(m_old[h] - m_new[h]) for h in hs]
        one = jnp.ones((16, FK), bf16)
        v_one = [
            jnp.concatenate([kvt_ref[128 * h + HEAD_DIM : 128 * (h + 1), rows], one], axis=0)
            for h in hs
        ]
        out = [mm(v_one[h], p[h]) for h in hs]
        for h in hs:
            own = slice(HEAD_DIM * h, HEAD_DIM * (h + 1))
            acc_sc[own, :] = acc_sc[own, :] * fade[h] + out[h][:HEAD_DIM]
            l_sc[h : h + 1, :] = fade[h] * l_old[h] + out[h][HEAD_DIM : HEAD_DIM + 1]
            m_sc[h : h + 1, :] = m_new[h]
        return carry

    lax.fori_loop(span[i, 0], span[i, 1], step, 0)
    for h in range(OWN_HEADS):
        own = slice(HEAD_DIM * h, HEAD_DIM * (h + 1))
        total = l_sc[h : h + 1, :]
        ot_ref[own, :] = (acc_sc[own, :] / total).astype(bf16)
        lse_ref[h : h + 1, :] = m_sc[h : h + 1, :] + jnp.log(total)
    lse_ref[OWN_HEADS:, :] = jnp.zeros_like(lse_ref[OWN_HEADS:, :])


def attend(span, qtag, ktag, qt, kv, kvt):
    own = qt.shape[1]
    window = kv.shape[0]
    whole = lambda shape: pl.BlockSpec(shape, lambda i, s: (0, 0), pipeline_mode=pl.Buffered(1))
    cols = lambda rows: pl.BlockSpec((rows, BQ), lambda i, s: (0, i))
    return pl.pallas_call(
        attend_kernel,
        grid_spec=pltpu.PrefetchScalarGridSpec(
            num_scalar_prefetch=1,
            grid=(own // BQ,),
            in_specs=[
                cols(1),
                whole((window, 1)),
                cols(Q_ROWS),
                whole((window, KV_ROWS)),
                whole((KV_ROWS, window)),
            ],
            out_specs=[cols(Q_ROWS), cols(8)],
            scratch_shapes=[
                pltpu.VMEM((8, BQ), f32),
                pltpu.VMEM((8, BQ), f32),
                pltpu.VMEM((Q_ROWS, BQ), f32),
            ],
        ),
        out_shape=[
            jax.ShapeDtypeStruct((Q_ROWS, own), bf16),
            jax.ShapeDtypeStruct((8, own), f32),
        ],
        compiler_params=pltpu.CompilerParams(vmem_limit_bytes=60 << 20),
        cost_estimate=pl.CostEstimate(
            flops=4 * own * 2048 * Q_ROWS, bytes_accessed=20 << 20, transcendentals=own * 6144
        ),
        name="attend",
    )(span, qtag, ktag, qt, kv, kvt)


def grad_kernel(
    parts, final, span, qtag_ref, ktag_ref, qt_ref, dot_ref, ot_ref, lse_ref, kv_ref, kvt_ref, *rest
):
    if final:
        dq_in, dq_ref, *rest = rest
    else:
        dq_in, (dq_ref, *rest) = None, rest
    outs, (dq_sc, dkv_sc) = rest[: len(parts)], rest[len(parts) :]
    i = pl.program_id(0)

    @pl.when(i == 0)
    def _():
        dkv_sc[...] = jnp.zeros_like(dkv_sc)

    if final:
        dq_sc[...] = dq_in[...]
    else:
        dq_sc[...] = jnp.zeros_like(dq_sc)
    qtag = qtag_ref[...]
    qt, d_out, out = qt_ref[...], dot_ref[...], ot_ref[...]
    q_pad = [head_rows(qt, h, False) for h in range(OWN_HEADS)]
    d_pad = [head_rows(d_out, h, True) for h in range(OWN_HEADS)]
    product = d_out.astype(f32) * out.astype(f32)
    inner = [
        jnp.sum(product[HEAD_DIM * h : HEAD_DIM * (h + 1)], axis=0, keepdims=True)
        for h in range(OWN_HEADS)
    ]
    log_row = [lse_ref[h : h + 1, :] for h in range(OWN_HEADS)]

    def step(shift, kb, carry):
        rows = pl.ds(pl.multiple_of(kb * BK, BK), BK)
        place = pl.ds(pl.multiple_of((kb - shift) * BK, BK), BK)
        seen = ktag_ref[rows, :] == qtag
        hs = range(OWN_HEADS)
        kv = [kv_ref[rows, 128 * h : 128 * (h + 1)] for h in hs]
        s = [mm(kv[h], q_pad[h]) for h in hs]
        d_p = [mm(kv[h], d_pad[h]) for h in hs]
        p = [jnp.where(seen, jnp.exp(s[h] - log_row[h]), 0.0) for h in hs]
        d_s = [(p[h] * (d_p[h] - inner[h])).astype(bf16) for h in hs]
        p = [v.astype(bf16) for v in p]
        g_kv = [mm(q_pad[h], d_s[h], NT) + mm(d_pad[h], p[h], NT) for h in hs]
        g_q = [mm(kvt_ref[128 * h : 128 * h + HEAD_DIM, rows], d_s[h]) for h in hs]
        for h in hs:
            dkv_sc[128 * h : 128 * (h + 1), place] += g_kv[h]
            own = slice(HEAD_DIM * h, HEAD_DIM * (h + 1))
            dq_sc[own, :] += g_q[h]
        return carry

    base = 0
    for n, (first, last) in enumerate(parts):
        low = jnp.maximum(span[i, 0], first)
        high = jnp.minimum(span[i, 1], last)
        lax.fori_loop(low, high, functools.partial(step, first - base), 0)
        base += last - first
    if final:
        dq_ref[...] = (dq_sc[...] * score_scale).astype(bf16)
    else:
        dq_ref[...] = dq_sc[...]

    @pl.when(i == pl.num_programs(0) - 1)
    def _():
        base = 0
        for (first, last), ref in zip(parts, outs):
            width = (last - first) * BK
            ref[...] = dkv_sc[:, base : base + width].astype(ref.dtype)
            base += width


def attend_grad(parts, final, span, qtag, ktag, qt, d_out, out, lse, kv, kvt, dq_in=None):
    own = qt.shape[1]
    window = kv.shape[0]
    whole = lambda shape: pl.BlockSpec(shape, lambda i, s: (0, 0), pipeline_mode=pl.Buffered(1))
    cols = lambda rows: pl.BlockSpec((rows, BQ), lambda i, s: (0, i))
    widths = [(last - first) * BK for first, last in parts]
    dtype = f32 if final else bf16
    args = [span, qtag, ktag, qt, d_out, out, lse, kv, kvt] + ([dq_in] if final else [])
    return pl.pallas_call(
        functools.partial(grad_kernel, parts, final),
        grid_spec=pltpu.PrefetchScalarGridSpec(
            num_scalar_prefetch=1,
            grid=(own // BQ,),
            in_specs=[
                cols(1),
                whole((window, 1)),
                cols(Q_ROWS),
                cols(Q_ROWS),
                cols(Q_ROWS),
                cols(8),
                whole((window, KV_ROWS)),
                whole((KV_ROWS, window)),
            ]
            + ([cols(Q_ROWS)] if final else []),
            out_specs=[cols(Q_ROWS)] + [whole((KV_ROWS, w)) for w in widths],
            scratch_shapes=[
                pltpu.VMEM((Q_ROWS, BQ), f32),
                pltpu.VMEM((KV_ROWS, sum(widths)), f32),
            ],
        ),
        out_shape=[jax.ShapeDtypeStruct((Q_ROWS, own), bf16 if final else f32)]
        + [jax.ShapeDtypeStruct((KV_ROWS, w), dtype) for w in widths],
        compiler_params=pltpu.CompilerParams(vmem_limit_bytes=60 << 20),
        cost_estimate=pl.CostEstimate(
            flops=(10 if final else 2) * own * 1536 * Q_ROWS,
            bytes_accessed=20 << 20,
            transcendentals=own * 4096,
        ),
        name="grad_own" if final else "grad_far",
    )(*args)


MESH = pl.DeviceIdType.MESH
CHUNKS = 8
W_LANES = 640
KV_AT = 256


def remote(src, dst, send, recv, target):
    return pltpu.make_async_remote_copy(
        src_ref=src,
        dst_ref=dst,
        send_sem=send,
        recv_sem=recv,
        device_id=(target,),
        device_id_type=MESH,
    )


def share_kernel(
    n_dev, rows_w, tok_ref, code_ref, w_ref, x_own, c_out, w_turn, qt_out, kv_out, kvt_out,
    x_out, w_out, w_wide, w_full, qt_sc, kv_sc, kvt_sc,
    w_send, w_recv, c_send, c_recv, part_send, part_recv, mate_send, mate_recv,
    up_send, up_recv, down_send, down_recv, cross_send, cross_recv,
    fwd_send, fwd_recv, keep_sem, x_sem, q_sem, kv_sem, kvt_sem,
):
    n_group = n_dev // GROUP
    me = lax.axis_index("fsdp")
    g = me // GROUP
    s = me % GROUP
    k = s % 2
    hi = s // 2
    partner = me + 1 - 2 * k
    mate = me + 2 - 4 * hi
    mate_block = 4 + k - 2 * hi
    has_up = g < n_group - 1
    has_down = g > 0
    rows = tok_ref.shape[0] // CHUNKS
    half = CHUNKS // 2

    barrier = pltpu.get_barrier_semaphore()

    def greet(r, carry):
        pl.semaphore_signal(
            barrier, inc=1, device_id=(lax.rem(me + r, n_dev),), device_id_type=MESH
        )
        return carry

    lax.fori_loop(1, n_dev, greet, 0)
    pl.semaphore_wait(barrier, n_dev - 1)

    def chunk(ref, c):
        return ref.at[pl.ds(pl.multiple_of(c * rows, rows), rows)]

    def spot(b, c):
        return x_out.at[b, pl.ds(pl.multiple_of(c * rows, rows), rows)]

    def to_partner(c):
        return remote(chunk(tok_ref, c), spot(2 + s, c), part_send.at[c], part_recv.at[c], partner)

    def to_mate(c):
        return remote(chunk(tok_ref, c), spot(2 + s, c), mate_send.at[c], mate_recv.at[c], mate)

    def up_own(c):
        return remote(chunk(tok_ref, c), spot(k, c), up_send.at[c], up_recv.at[c], me + GROUP)

    def up_mate(c):
        return remote(spot(mate_block, c), spot(k, c), up_send.at[c], up_recv.at[c], me + GROUP)

    def down_own(c):
        return remote(
            chunk(tok_ref, c), spot(6 + k, c), down_send.at[c], down_recv.at[c], me - GROUP
        )

    def down_mate(c):
        return remote(
            spot(mate_block, c + half), spot(6 + k, c + half), down_send.at[c], down_recv.at[c],
            me - GROUP,
        )

    def cross(c):
        at = c + half * hi
        return remote(spot(6 + k, at), spot(6 + k, at), cross_send.at[c], cross_recv.at[c], mate)

    def forward(b, c, slot):
        return remote(spot(b, c), spot(b, c), fwd_send.at[slot], fwd_recv.at[slot], partner)

    keep_x = pltpu.make_async_copy(tok_ref, x_out.at[2 + s], keep_sem.at[0])
    keep_c = pltpu.make_async_copy(code_ref, c_out.at[2 + s], keep_sem.at[1])
    keep_w = pltpu.make_async_copy(w_ref.at[s], w_out.at[me], keep_sem.at[2])
    keep_x.start()
    keep_c.start()
    keep_w.start()

    def w_copy(r):
        target = lax.rem(me + r, n_dev)
        return remote(
            w_ref.at[lax.rem(target, GROUP)], w_out.at[me], w_send.at[r], w_recv.at[r], target
        )

    def w_start(r, carry):
        w_copy(r).start()
        return carry

    def c_group(j):
        target = GROUP * g + lax.rem(s + j, GROUP)
        return remote(code_ref, c_out.at[2 + s], c_send.at[j], c_recv.at[2 + s], target)

    def c_far(j):
        step = GROUP * (2 * hi - 1)
        b = 6 + s - 8 * hi
        target = GROUP * g + step + j
        return remote(code_ref, c_out.at[b], c_send.at[GROUP + j], c_recv.at[b], target)

    sends_far = jnp.where(hi == 1, g < n_group - 1, g > 0)
    for j in range(1, GROUP):
        c_group(j).start()

    @pl.when(sends_far)
    def _():
        for j in range(GROUP):
            c_far(j).start()

    order = list(range(half, CHUNKS)) + list(range(half))
    lax.fori_loop(1, n_dev, w_start, 0)

    @pl.when((hi == 0) & has_down)
    def _():
        for c in range(half):
            down_own(c).start()

    for n, c in enumerate(order):
        to_mate(c).start()
        to_partner(c).start()
        if n < half:

            @pl.when((hi == 1) & has_up)
            def _():
                up_own(c).start()

    for n, c in enumerate(order):
        to_mate(c).wait_recv()
        forward(mate_block, c, c).start()

        @pl.when((hi == 0) & has_up)
        def _():
            up_mate(c).start()

        if n < half:

            @pl.when((hi == 1) & has_down)
            def _():
                down_mate(c - half).start()

        else:

            @pl.when((hi == 1) & has_up)
            def _():
                up_own(c).start()

    def w_wait(r, carry):
        w_copy(r).wait_recv()
        return carry

    lax.fori_loop(1, n_dev, w_wait, 0)
    keep_w.wait()
    keep_x.wait()
    bias_row = jnp.zeros((8, W_LANES), f32)
    bias_at = w_ref.shape[1] - 8
    for j in range(n_dev):
        w_wide[rows_w * j : rows_w * (j + 1), :] = w_out[j, :rows_w, :].astype(f32)
        bias_row = bias_row + w_out[j, bias_at:, :].astype(f32)
    bias_row = jnp.sum(bias_row, axis=0, keepdims=True)
    bias_col = jnp.broadcast_to(bias_row, (128, W_LANES)).T[:, :1]
    w_full[...] = w_wide[...].astype(bf16)
    w_turn[...] = w_wide[...].T.astype(bf16)
    piece = 512
    pieces = tok_ref.shape[0] // piece

    def project(b, inside):
        def one(j, carry):
            x = x_out[b, pl.ds(pl.multiple_of(j * piece, piece), piece), :]
            at = pl.ds(pl.multiple_of((b * pieces + j) * piece, piece), piece)
            kv = mm(x, w_full[:, KV_AT:]) + bias_row[:, KV_AT:]
            kv_sc[at, :] = kv.astype(bf16)
            kvt_sc[:, at] = (mm(w_turn[KV_AT:, :], x, NT) + bias_col[KV_AT:]).astype(bf16)
            if inside:
                to = pl.ds(pl.multiple_of(((b - 2) * pieces + j) * piece, piece), piece)
                q = (mm(w_turn[:Q_ROWS, :], x, NT) + bias_col[:Q_ROWS]).astype(bf16)
                qt_sc[:, to] = q * jnp.asarray(score_scale, bf16)
            return carry

        lax.fori_loop(0, pieces, one, 0)

    def outs(b, inside):
        whole = tok_ref.shape[0]
        at = pl.ds(pl.multiple_of(b * whole, whole), whole)
        copies = [
            pltpu.make_async_copy(kv_sc.at[at], kv_out.at[at], kv_sem.at[b]),
            pltpu.make_async_copy(kvt_sc.at[:, at], kvt_out.at[:, at], kvt_sem.at[b]),
        ]
        if inside:
            to = pl.ds(pl.multiple_of((b - 2) * whole, whole), whole)
            copies.append(pltpu.make_async_copy(qt_sc.at[:, to], qt_out.at[:, to], q_sem.at[b - 2]))
            copies.append(pltpu.make_async_copy(x_out.at[b], x_own.at[b - 2], x_sem.at[b - 2]))
        return copies

    def put(b, inside):
        for copy in outs(b, inside):
            copy.start()

    own_block = 2 + s
    near_block = own_block + 1 - 2 * k
    across_block = mate_block + 1 - 2 * k
    project(own_block, True)

    @pl.when(has_up)
    def _():
        for c in range(half):
            down_own(c).wait_recv()
            cross(c).start()
            forward(6 + k, c + half * hi, 2 * CHUNKS + c).start()

    project(mate_block, True)
    put(own_block, True)

    @pl.when(has_down)
    def _():
        for c in order:
            up_own(c).wait_recv()
            forward(k, c, CHUNKS + c).start()

    for c in range(CHUNKS):
        to_partner(c).wait_recv()
    project(near_block, True)
    put(mate_block, True)

    @pl.when(has_up)
    def _():
        for c in range(half):
            cross(c).wait_recv()
            forward(6 + k, c + half * (1 - hi), 2 * CHUNKS + half + c).start()

    for c in range(CHUNKS):
        forward(mate_block, c, c).wait_recv()
    project(across_block, True)
    put(near_block, True)

    @pl.when(has_down)
    def _():
        project(k, False)
        for c in range(CHUNKS):
            forward(k, c, CHUNKS + c).wait_recv()
        project(1 - k, False)
        put(k, False)

    put(across_block, True)

    @pl.when(has_up)
    def _():
        project(6 + k, False)
        for c in range(half):
            forward(6 + k, c, 2 * CHUNKS + c).wait_recv()
            forward(6 + k, c, 2 * CHUNKS + half + c).wait_recv()
        project(7 - k, False)
        put(6 + k, False)

    for c in range(CHUNKS):
        to_partner(c).wait_send()
        to_mate(c).wait_send()
        forward(mate_block, c, c).wait_send()

    @pl.when(has_down)
    def _():
        put(1 - k, False)
        for c in range(CHUNKS):
            forward(k, c, CHUNKS + c).wait_send()
        for c in range(half):
            down_own(c).wait_send()

    @pl.when(has_up)
    def _():
        for c in range(half):
            cross(c).wait_send()
            forward(6 + k, c, 2 * CHUNKS + c).wait_send()
            forward(6 + k, c, 2 * CHUNKS + half + c).wait_send()
        for c in range(CHUNKS):
            up_own(c).wait_send()
        put(7 - k, False)

    for j in range(1, GROUP):
        c_group(j).wait_send()
        remote(
            code_ref, c_out.at[0], c_send.at[j], c_recv.at[2 + lax.rem(s + j, GROUP)], partner
        ).wait_recv()

    @pl.when(sends_far)
    def _():
        for j in range(GROUP):
            c_far(j).wait_send()

    @pl.when(has_down)
    def _():
        for b in range(2):
            remote(code_ref, c_out.at[b], c_send.at[0], c_recv.at[b], partner).wait_recv()

    @pl.when(has_up)
    def _():
        for b in range(6, 8):
            remote(code_ref, c_out.at[b], c_send.at[0], c_recv.at[b], partner).wait_recv()

    def w_sent(r, carry):
        w_copy(r).wait_send()
        return carry

    lax.fori_loop(1, n_dev, w_sent, 0)
    keep_c.wait()
    for b in range(2, 6):
        for copy in outs(b, True):
            copy.wait()

    @pl.when(has_down)
    def _():
        for b in range(2):
            for copy in outs(b, False):
                copy.wait()

    @pl.when(has_up)
    def _():
        for b in range(6, 8):
            for copy in outs(b, False):
                copy.wait()


def share(n_dev, rows_w, tokens, code, w_send):
    vmem = pl.BlockSpec(memory_space=pltpu.VMEM)
    anywhere = pl.BlockSpec(memory_space=pl.ANY)
    dma = lambda n: pltpu.SemaphoreType.DMA((n,))
    half = CHUNKS // 2
    rows, width = tokens.shape
    own, window = GROUP * rows, 8 * rows
    return pl.pallas_call(
        functools.partial(share_kernel, n_dev, rows_w),
        in_specs=[vmem] * 3,
        out_specs=[anywhere, anywhere, vmem, anywhere, anywhere, anywhere],
        out_shape=[
            jax.ShapeDtypeStruct((GROUP, rows, width), bf16),
            jax.ShapeDtypeStruct((8,) + code.shape, code.dtype),
            jax.ShapeDtypeStruct((W_LANES, width), bf16),
            jax.ShapeDtypeStruct((Q_ROWS, own), bf16),
            jax.ShapeDtypeStruct((window, KV_ROWS), bf16),
            jax.ShapeDtypeStruct((KV_ROWS, window), bf16),
        ],
        scratch_shapes=[
            pltpu.VMEM((8, rows, width), bf16),
            pltpu.VMEM((n_dev,) + w_send.shape[1:], bf16),
            pltpu.VMEM((width, W_LANES), f32),
            pltpu.VMEM((width, W_LANES), bf16),
            pltpu.VMEM((Q_ROWS, own), bf16),
            pltpu.VMEM((window, KV_ROWS), bf16),
            pltpu.VMEM((KV_ROWS, window), bf16),
            dma(n_dev), dma(n_dev), dma(2 * GROUP), dma(8),
            dma(CHUNKS), dma(CHUNKS), dma(CHUNKS), dma(CHUNKS),
            dma(CHUNKS), dma(CHUNKS), dma(half), dma(half), dma(half), dma(half),
            dma(3 * CHUNKS), dma(3 * CHUNKS), dma(3), dma(GROUP), dma(GROUP), dma(8), dma(8),
        ],
        compiler_params=pltpu.CompilerParams(
            collective_id=0, has_side_effects=True, vmem_limit_bytes=60 << 20
        ),
        name="share",
    )(tokens, code, w_send)


PARTS = 4
TN = (((0,), (0,)), ((), ()))


def settle_kernel(
    n_dev, rows_w, mix_ref, x_ref, w_ref, vec_ref, own_out, near_out, far_out, w_out, vec_out,
    wide, slabs, across, near, relay, total,
    w_send, w_recv, vec_send, vec_recv, near_send, near_recv, relay_send, relay_recv,
    far_send, far_recv, keep_sem,
):
    me = lax.axis_index("fsdp")
    s = me % GROUP
    k = s % 2
    hi = s // 2
    partner = me + 1 - 2 * k
    mate = me + 2 - 4 * hi
    s_partner = s + 1 - 2 * k
    s_mate = s + 2 - 4 * hi
    s_across = 3 - s
    block = own_out.shape[0]
    rows = block // PARTS

    barrier = pltpu.get_barrier_semaphore()

    def greet(r, carry):
        pl.semaphore_signal(
            barrier, inc=1, device_id=(lax.rem(me + r, n_dev),), device_id_type=MESH
        )
        return carry

    lax.fori_loop(1, n_dev, greet, 0)
    pl.semaphore_wait(barrier, n_dev - 1)

    def part(c):
        return pl.ds(c * rows, rows)

    def to_relay(c):
        return remote(
            across.at[part(c)], relay.at[part(c)], relay_send.at[c], relay_recv.at[c], partner
        )

    def to_near(c):
        return remote(
            near.at[part(c)], near_out.at[part(c)], near_send.at[c], near_recv.at[c], partner
        )

    def to_far(c):
        return remote(total.at[part(c)], far_out.at[part(c)], far_send.at[c], far_recv.at[c], mate)

    def w_copy(r):
        target = lax.rem(me + r, n_dev)
        return remote(slabs.at[target], w_out.at[me], w_send.at[r], w_recv.at[r], target)

    def vec_copy(r):
        target = lax.rem(me + r, n_dev)
        return remote(vec_ref.at[target], vec_out.at[me], vec_send.at[r], vec_recv.at[r], target)

    def vec_start(r, carry):
        vec_copy(r).start()
        return carry

    lax.fori_loop(1, n_dev, vec_start, 0)
    keep_vec = pltpu.make_async_copy(vec_ref.at[me], vec_out.at[me], keep_sem.at[1])
    keep_vec.start()

    wide[...] = jnp.zeros_like(wide)

    def add_rows(j, carry):
        at = pl.ds(pl.multiple_of(j * block, block), block)
        wide[:MIX_ROWS, :] += mm(mix_ref[:, at], x_ref[at, :])
        return carry

    lax.fori_loop(0, GROUP, add_rows, 0)
    turned = wide[...].T.astype(bf16).astype(f32)
    bias = mm(jnp.ones((8, GROUP * block), bf16), mix_ref[...], NT).astype(bf16)
    bias_at = slabs.shape[1] - 8
    for j in range(n_dev):
        slabs[j, :rows_w, :] = turned[rows_w * j : rows_w * (j + 1), :].astype(bf16)
        slabs[j, bias_at:, :MIX_ROWS] = bias

    def back(t, c):
        at = pl.ds(pl.multiple_of(t * block + c * rows, rows), rows)
        return mm(mix_ref[:, at], w_ref[...], TN)

    for c in range(PARTS):
        across[c * rows : (c + 1) * rows, :] = back(s_across, c).astype(bf16)
        if c > 0:
            to_relay(c - 1).start()

    def w_start(r, carry):
        w_copy(r).start()
        return carry

    lax.fori_loop(1, n_dev, w_start, 0)
    keep_w = pltpu.make_async_copy(slabs.at[me], w_out.at[me], keep_sem.at[0])
    keep_w.start()
    mine = back(s_mate, 0)
    to_relay(PARTS - 1).start()
    for c in range(PARTS):
        to_relay(c).wait_recv()
        other = relay[c * rows : (c + 1) * rows, :].astype(f32)
        total[c * rows : (c + 1) * rows, :] = (mine + other).astype(bf16)
        if c + 1 < PARTS:
            mine = back(s_mate, c + 1)
        else:
            near[:rows, :] = back(s_partner, 0).astype(bf16)
        to_far(c).start()
    for c in range(1, PARTS):
        near[c * rows : (c + 1) * rows, :] = back(s_partner, c).astype(bf16)
        to_near(c - 1).start()
    for c in range(PARTS):
        own_out[c * rows : (c + 1) * rows, :] = back(s, c)
        if c == 0:
            to_near(PARTS - 1).start()
    for c in range(PARTS):
        to_relay(c).wait_send()
        to_near(c).wait()
        to_far(c).wait()

    def finish(r, carry):
        w_copy(r).wait()
        vec_copy(r).wait()
        return carry

    lax.fori_loop(1, n_dev, finish, 0)
    keep_w.wait()
    keep_vec.wait()


def settle(n_dev, rows_w, mix, x, w, vec):
    vmem = pl.BlockSpec(memory_space=pltpu.VMEM)
    anywhere = pl.BlockSpec(memory_space=pl.ANY)
    dma = lambda n: pltpu.SemaphoreType.DMA((n,))
    block = (x.shape[0] // GROUP, x.shape[1])
    slabs = (n_dev, rows_w + -rows_w % 8 + 8, W_LANES)
    return pl.pallas_call(
        functools.partial(settle_kernel, n_dev, rows_w),
        in_specs=[vmem] * 4,
        out_specs=[vmem] + [anywhere] * 4,
        out_shape=[
            jax.ShapeDtypeStruct(block, f32),
            jax.ShapeDtypeStruct(block, bf16),
            jax.ShapeDtypeStruct(block, bf16),
            jax.ShapeDtypeStruct(slabs, bf16),
            jax.ShapeDtypeStruct(vec.shape, vec.dtype),
        ],
        scratch_shapes=[
            pltpu.VMEM((W_LANES, x.shape[1]), f32),
            pltpu.VMEM(slabs, bf16),
            pltpu.VMEM(block, bf16), pltpu.VMEM(block, bf16),
            pltpu.VMEM(block, bf16), pltpu.VMEM(block, bf16),
            dma(n_dev), dma(n_dev), dma(n_dev), dma(n_dev),
            dma(PARTS), dma(PARTS), dma(PARTS), dma(PARTS), dma(PARTS), dma(PARTS), dma(2),
        ],
        compiler_params=pltpu.CompilerParams(
            collective_id=1, has_side_effects=True, vmem_limit_bytes=60 << 20
        ),
        name="settle",
    )(mix, x, w, vec)


def body(
    n_dev,
    tokens,
    segment_ids,
    pad_mask,
    w_qkv,
    bias_query,
    bias_value,
    w_out,
    bias_out,
    gain_one,
    shift_one,
    w_up,
    bias_up,
    w_down,
    bias_down,
    gain_two,
    shift_two,
    cotangent,
):
    row_count = tokens.shape[0]
    rows_w = w_qkv.shape[0]
    own = GROUP * row_count
    window = own + 2 * LEN_MAX
    me = lax.axis_index("fsdp")
    place = me % GROUP
    group_id = me // GROUP
    n_group = n_dev // GROUP
    up = [(i, i + GROUP) for i in range(n_dev - GROUP)]
    down = [(i + GROUP, i) for i in range(n_dev - GROUP)]
    groups = [[GROUP * g + j for j in range(GROUP)] for g in range(n_group)]

    wq = w_qkv[:, :D].reshape(rows_w, GROUP, Q_ROWS)
    wk = w_qkv[:, D : 2 * D].reshape(rows_w, GROUP, OWN_HEADS, 1, HEAD_DIM)
    wv = w_qkv[:, 2 * D :].reshape(rows_w, GROUP, OWN_HEADS, 1, HEAD_DIM)
    wkv = jnp.concatenate([wk, wv], axis=3).reshape(rows_w, GROUP, KV_ROWS)
    gap = KV_AT - Q_ROWS
    lane = jnp.arange(gap)[None, :]
    small_cols = jnp.pad(bias_up.reshape(rows_w, -1), ((0, 0), (6, gap - 10)))
    for j, v in enumerate([bias_out, gain_one, shift_one, bias_down, gain_two, shift_two]):
        small_cols = jnp.where(lane == j, v[:, None], small_cols)
    small_cols = jnp.broadcast_to(small_cols[:, None], (rows_w, GROUP, gap))
    w_cut = jnp.concatenate([wq, small_cols, wkv], axis=2).transpose(1, 0, 2)
    column = me * rows_w + jnp.arange(rows_w)
    feature = jnp.arange(D)
    spread = lambda bias: jnp.sum(
        jnp.where(feature[None] == column[:, None], bias.astype(f32)[:, None], 0.0), axis=0
    )
    bias_q = spread(bias_query).reshape(GROUP, Q_ROWS)
    bias_v = spread(bias_value).reshape(GROUP, OWN_HEADS, 1, HEAD_DIM)
    bias_kv = jnp.concatenate([jnp.zeros_like(bias_v), bias_v], axis=2).reshape(GROUP, KV_ROWS)
    bias_cut = jnp.concatenate([bias_q, jnp.zeros((GROUP, gap), f32), bias_kv], axis=1)
    fill = -rows_w % 8
    bias_cut = jnp.pad(bias_cut.astype(bf16)[:, None], ((0, 0), (fill, 7), (0, 0)))
    w_send = jnp.concatenate([w_cut, bias_cut], axis=1)
    ff = w_up.shape[1]
    wo_full = lax.all_gather(w_out, "fsdp", axis=0, tiled=True)
    wu_full = lax.all_gather(w_up, "fsdp", axis=0, tiled=True)
    wd_full = lax.all_gather(w_down, "fsdp", axis=0, tiled=True)

    code = (segment_ids * 2 + pad_mask).reshape(8, row_count // 8)
    x_own, code_win, w_turn, qt, kv, kvt = share(n_dev, rows_w, tokens, code, w_send)
    x_own = x_own.reshape(own, D)
    code_win = code_win.reshape(window)
    at = jnp.arange(window)
    code_win = jnp.where((group_id == 0) & (at < LEN_MAX), -2, code_win)
    code_win = jnp.where(
        (group_id == n_group - 1) & (at >= LEN_MAX + own), 2 * n_dev * row_count, code_win
    )
    code_own = code_win[LEN_MAX : LEN_MAX + own]
    w_back = jnp.concatenate([w_turn[:Q_ROWS], w_turn[KV_AT:]], axis=0)
    small_all = w_turn[Q_ROWS : Q_ROWS + 10].astype(f32)
    bu_full = small_all[6:].T.reshape(-1)
    bo_full, g1_full, s1_full, bd_full, g2_full, s2_full = [small_all[j] for j in range(6)]
    seg_win = code_win >> 1
    ktag = jnp.where((code_win & 1) == 1, seg_win + 1, 0).reshape(window, 1)
    seg_own = code_own >> 1
    qtag = (seg_own + 1).reshape(1, own)
    first_seg = seg_own[::BQ]
    last_seg = seg_own[BQ - 1 :: BQ]
    low = jnp.sum((seg_win[None, :] < first_seg[:, None]).astype(jnp.int32), axis=1)
    high = jnp.sum((seg_win[None, :] <= last_seg[:, None]).astype(jnp.int32), axis=1)
    spans = [jnp.stack([low // b, (high + b - 1) // b], axis=1) for b in (FK, BK)]

    ot, lse = attend(spans[0], qtag, ktag, qt, kv, kvt)
    ctx_t = lax.all_to_all(
        ot.reshape(Q_ROWS, GROUP, row_count), "fsdp", 1, 0, axis_index_groups=groups, tiled=True
    ).reshape(D, row_count)

    tokens_f = tokens.astype(f32)
    branch = jnp.einsum("ir,io->ro", ctx_t, wo_full, preferred_element_type=f32) + bo_full
    first, norm_one_back = jax.vjp(norm_rows, tokens_f + branch, g1_full, s1_full)
    up_in = first.astype(bf16)
    pre_act = jnp.dot(up_in, wu_full, preferred_element_type=f32) + bu_full
    gelu_val, gelu_back = jax.vjp(gelu_exact, pre_act)
    hidden = gelu_val.astype(bf16)
    ffn = jnp.dot(hidden, wd_full, preferred_element_type=f32) + bd_full
    result, norm_two_back = jax.vjp(norm_rows, first + ffn, g2_full, s2_full)
    layer_out = result.astype(bf16)
    d_second, d_gain_two, d_shift_two = norm_two_back(cotangent.astype(f32))
    d_ffn = d_second.astype(bf16)
    d_bias_down = jnp.sum(d_ffn.astype(f32), axis=0)
    d_w_down = jnp.einsum("rf,rd->fd", hidden, d_ffn, preferred_element_type=f32)
    d_hidden = jnp.einsum("rd,fd->rf", d_ffn, wd_full, preferred_element_type=f32)
    d_pre = gelu_back(d_hidden)[0].astype(bf16)
    d_bias_up = jnp.sum(d_pre.astype(f32), axis=0)
    d_w_up = [
        jnp.einsum("rd,rf->df", up_in, d_pre[:, D * j : D * (j + 1)], preferred_element_type=f32)
        for j in range(ff // D)
    ]
    d_first = d_second + jnp.einsum("rf,df->rd", d_pre, wu_full, preferred_element_type=f32)
    d_mid, d_gain_one, d_shift_one = norm_one_back(d_first)
    d_branch = d_mid.astype(bf16)
    d_bias_out = jnp.sum(d_branch.astype(f32), axis=0)
    d_w_out = jnp.einsum("ir,ro->io", ctx_t, d_branch, preferred_element_type=f32)
    dctx_t = jnp.einsum("ro,io->ir", d_branch, wo_full, preferred_element_type=f32).astype(bf16)
    n_up = ff // D
    big_grad = jnp.concatenate(
        [
            d_w_down.astype(bf16).reshape(n_dev, -1, D),
            d_w_out.astype(bf16).reshape(n_dev, rows_w, D),
        ]
        + [v.astype(bf16).reshape(n_dev, rows_w, D) for v in d_w_up],
        axis=1,
    )
    big_owned = lax.psum_scatter(big_grad, "fsdp", scatter_dimension=0).astype(f32)
    rows_d = w_down.shape[0]
    g_down, g_out = big_owned[:rows_d], big_owned[rows_d : rows_d + rows_w]
    g_up = jnp.concatenate(
        [big_owned[rows_d + rows_w * (j + 1) : rows_d + rows_w * (j + 2)] for j in range(n_up)], axis=1
    )

    d_out = lax.all_to_all(
        dctx_t.reshape(GROUP, Q_ROWS, row_count), "fsdp", 0, 2, axis_index_groups=groups, tiled=True
    ).reshape(Q_ROWS, own)
    edge, inside = LEN_MAX // BK, own // BK
    far_parts = ((0, edge), (edge + inside, 2 * edge + inside))
    own_parts = ((edge, edge + inside),)
    dq_far, dkv_left, dkv_right = attend_grad(
        far_parts, False, spans[1], qtag, ktag, qt, d_out, ot, lse, kv, kvt
    )
    from_right = lax.ppermute(dkv_left, "fsdp", down)
    from_left = lax.ppermute(dkv_right, "fsdp", up)
    dq_t, dkv_own = attend_grad(
        own_parts, True, spans[1], qtag, ktag, qt, d_out, ot, lse, kv, kvt, dq_far
    )
    dkv = jnp.concatenate(
        [
            dkv_own[:, :LEN_MAX] + from_left.astype(f32),
            dkv_own[:, LEN_MAX : own - LEN_MAX],
            dkv_own[:, own - LEN_MAX :] + from_right.astype(f32),
        ],
        axis=1,
    ).astype(bf16)
    dmix_t = jnp.concatenate([dq_t, dkv], axis=0)
    vecs = jnp.stack([d_bias_out, d_gain_one, d_shift_one, d_bias_down, d_gain_two, d_shift_two])
    vec_send = jnp.concatenate(
        [
            vecs.reshape(6, n_dev, rows_w).transpose(1, 0, 2).reshape(n_dev, 6 * rows_w),
            d_bias_up.reshape(n_dev, 4 * rows_w),
        ],
        axis=1,
    )
    vec_send = jnp.pad(vec_send, ((0, 0), (0, 1024 - vec_send.shape[1]))).reshape(n_dev, 8, 128)
    own_x, near, far, w_got, vec_got = settle(n_dev, rows_w, dmix_t, x_own, w_back, vec_send)
    grad_tokens = d_mid + ((own_x + near.astype(f32)) + far.astype(f32))
    got = jnp.sum(w_got.astype(f32).reshape(n_group, GROUP, -1, W_LANES), axis=0)
    got_q = got[:, :, :Q_ROWS].transpose(1, 0, 2).reshape(-1, D)
    got_kv = got[:, :, Q_ROWS:MIX_ROWS].transpose(1, 0, 2)
    got_kv = got_kv.reshape(-1, GROUP, OWN_HEADS, 2, HEAD_DIM)
    got_k = got_kv[:, :, :, 0].reshape(-1, D)
    got_v = got_kv[:, :, :, 1].reshape(-1, D)
    grad_w_qkv = jnp.concatenate([got_q[:rows_w], got_k[:rows_w], got_v[:rows_w]], axis=1)
    mine = lambda rows: lax.dynamic_slice(rows[-1], (me * rows_w,), (rows_w,))
    vec = jnp.sum(vec_got, axis=0).reshape(-1)[: 10 * rows_w]
    own_vec = [mine(got_q), mine(got_v)] + [vec[j * rows_w : (j + 1) * rows_w] for j in range(6)]
    return (
        layer_out,
        grad_tokens,
        grad_w_qkv,
        own_vec[0],
        own_vec[1],
        g_out,
        own_vec[2],
        own_vec[3],
        own_vec[4],
        g_up,
        vec[6 * rows_w :],
        g_down,
        own_vec[5],
        own_vec[6],
        own_vec[7],
    )


def solution(mesh):
    rows, flat = P("fsdp", None), P("fsdp")
    return jax.shard_map(
        functools.partial(body, mesh.shape["fsdp"]),
        mesh=mesh,
        in_specs=(
            rows, flat, flat, rows, flat, flat, rows, flat, flat, flat, rows, flat, rows, flat,
            flat, flat, rows,
        ),
        out_specs=(
            rows, rows, rows, flat, flat, rows, flat, flat, flat, rows, flat, rows, flat, flat,
            flat,
        ),
        check_vma=False,
    )
```

profile of v0, /device:TPU:0, one launch (start us, length us, event | category | flops | bytes accessed | tf_op | source)
XLA Modules:
  0.0 586.5 jit_solution(16843217417817567600)
XLA Ops:
  16.7 93.1 %share.1 = (bf16[4,1024,768]{2,1,0:T(8,128)(2,1)}, s32[8,8,128]{2,1,0:T(8,128)}, bf16[640,768]{1,0:T(8,128)(2,1)}, bf16[192,4096]{1,0:T(8,128)(2,1)}, bf16[8192,...) custom-call(bf16[1024,768]{1,0:T(8,128)(2,1)} %tok_ref.1, s32[8,128]{1,0:T(8,128)} %add_bitcast_fusion.code_ref, ...), custom_call_target="tpu_custom_call" | custom-call | tf_op jit(solution)/shard_map/share/pallas_call | solution.py:582
  112.4 3.4 copy.130
  115.8 4.9 add_select_fusion.ktag_ref
  120.7 65.1 %attend.1 = (bf16[192,4096]{1,0:T(8,128)(2,1)}, f32[8,4096]{1,0:T(8,128)}) custom-call(s32[8,2]{1,0:T(8,128)} %copy.131.span, s32[1,4096]{1,0:T(1,128)} %bitcast.138, s32[8192,1]{1,0:T(8,128)} %add_select_fusion.ktag_ref, bf16[192,4096]{1,0:T(8,128)(2,1)} %get-tuple-element.34.qt_ref, bf16[8192,384]{1,0:T(8,128)(2,1)} %get-tuple-element.35.kv_ref, ...), custom_call_target="tpu_custom_call" | custom-call | flops 6442450944 | bytes 20971520 | tf_op jit(solution)/shard_map/attend/pallas_call | solution.py:102
  185.8 2.7 copy.151
  188.5 3.6 all-to-all-start
  193.6 22.7 %all-to-all-done = bf16[192,4,1024]{2,0,1:T(8,128)(2,1)S(1)} async-done(((bf16[192,4,1024]{2,0,1:T(8,128)(2,1)}), bf16[192,4,1024]{2,0,1:T(8,128)(2,1)S(1)}, u32[]{:S(2)}, u32[]{:S(2)}) %all-to-all-start) | async-done | bytes 1572896 | tf_op jit(solution)/shard_map/all_to_all | solution.py:860
  217.4 4.2 fusion.41
  223.9 11.3 %multiply_convert_fusion = (bf16[1024,3072]{1,0:T(8,128)(2,1)}, f32[1024,3072]{1,0:T(8,128)}) fusion(f32[3072]{0:T(1024)S(1)} %add.212, bf16[1024,768]{1,0:T(8,128)(2,1)} %fusion.6, bf16[768,3072]{1,0:T(8,128)(2,1)} %all-gather.6.cloned.1.call-done), kind=kOutput, calls=%fused_computation.2 | convolution fusion | flops 4850712576 | bytes 25178112 | tf_op jit(solution)/shard_map/dot_general | solution.py:868
  235.2 3.9 all-gather.8.cloned.1.call-done
  239.1 8.8 %fusion.42 = (f32[1024]{0:T(1024)S(1)}, f32[1024,768]{1,0:T(8,128)S(1)}) fusion(f32[768]{0:T(1024)S(1)} %get-tuple-element.59, bf16[1024,3072]{1,0:T(8,128)(2,1)} %get-tuple-element.104, bf16[3072,768]{1,0:T(8,128)(2,1)} %all-gather.8.cloned.1.call-done, f32[768]{0:T(1024)S(1)} %get-tuple-element.60, f32[768]{0:T(1024)S(1)} %get-tuple-element.61, ...), kind=kOutput, calls=%fused_computation.155 | convolution fusion | flops 4837342208 | bytes 17323008 | tf_op jit(solution)/shard_map/dot_general | solution.py:871
  254.0 5.6 convolution_convert_fusion
  259.6 22.7 %convert_reduce_fusion = (f32[3072]{0:T(1024)S(1)}, bf16[1024,3072]{1,0:T(8,128)(2,1)S(1)}) fusion(bf16[1024,768]{1,0:T(8,128)(2,1)S(1)} %get-tuple-element.68, bf16[3072,768]{1,0:T(8,128)(2,1)S(1)} %bitcast.146, f32[1024,3072]{1,0:T(8,128)} %get-tuple-element.105, f32[3072]{0:T(1024)S(1)} %add.212), kind=kOutput, calls=%fused_computation | convolution fusion | flops 4882166784 | bytes 25190400 | tf_op jit(solution)/shard_map/rd,fd->rf/dot_general | solution.py:878
  286.5 3.0 fusion.18
  292.8 8.3 %multiply_reduce_fusion = (f32[768]{0:T(1024)S(1)}, f32[1024]{0:T(1024)S(1)}, f32[768]{0:T(1024)S(1)}, f32[1024,768]{1,0:T(8,128)S(1)}) fusion(f32[1024,768]{1,0:T(8,128)S(1)} %get-tuple-element.103, f32[1024]{0:T(1024)S(1)} %fusion.33, f32[1024]{0:T(1024)S(1)} %broadcast_multiply_fusion.1, f32[768]{0:T(1024)S(1)} %get-tuple-element.61, ...), kind=kOutput, calls=%fused_computation.23 | convolution fusion | flops 4839699456 | bytes 20472832 | tf_op jit(solution)/shard_map/rf,df->rd/dot_general | solution.py:885
  318.6 4.0 all-to-all-start.1
  325.0 17.6 %all-to-all-done.1 = bf16[4,192,1024]{2,1,0:T(8,128)(2,1)S(1)} async-done(((bf16[4,192,1024]{2,1,0:T(8,128)(2,1)}), bf16[4,192,1024]{2,1,0:T(8,128)(2,1)S(1)}, u32[]{:S(2)}, u32[]{:S(2)}) %all-to-all-start.1) | async-done | bytes 1572896 | tf_op jit(solution)/shard_map/all_to_all | solution.py:907
  345.6 21.3 %grad_far.1 = (f32[192,4096]{1,0:T(8,128)}, bf16[384,2048]{1,0:T(8,128)(2,1)}, bf16[384,2048]{1,0:T(8,128)(2,1)}) custom-call(s32[8,2]{1,0:T(8,128)} %copy.138.span, s32[1,4096]{1,0:T(1,128)} %bitcast.139, s32[8192,1]{1,0:T(8,128)} %add_select_fusion.ktag_ref, bf16[192,4096]{1,0:T(8,128)(2,1)} %get-tuple-element.34.qt_ref, bf16[192,4096]{1,0:T(8,128)(2,1)} %bitcast.126, ...), custom_call_target="tpu_custom_call" | custom-call | flops 2415919104 | bytes 20971520 | tf_op jit(solution)/shard_map/grad_far/pallas_call | solution.py:209
  366.9 4.3 collective-permute-start
  373.5 96.0 %grad_own.1 = (bf16[192,4096]{1,0:T(8,128)(2,1)}, f32[384,4096]{1,0:T(8,128)}) custom-call(s32[8,2]{1,0:T(8,128)} %copy.138.span, s32[1,4096]{1,0:T(1,128)} %bitcast.140, s32[8192,1]{1,0:T(8,128)} %add_select_fusion.ktag_ref, bf16[192,4096]{1,0:T(8,128)(2,1)} %get-tuple-element.34.qt_ref, bf16[192,4096]{1,0:T(8,128)(2,1)} %bitcast.127, ...), custom_call_target="tpu_custom_call" | custom-call | flops 12079595520 | bytes 20971520 | tf_op jit(solution)/shard_map/grad_own/pallas_call | solution.py:209
  469.6 4.1 add_convert_fusion.2
  473.7 8.7 %maximum_maximum_fusion.mix_ref = bf16[576,4096]{1,0:T(8,128)(2,1)} fusion(bf16[384,2048]{1,0:T(8,128)(2,1)S(1)} %get-tuple-element.78, bf16[384,2048]{1,0:T(8,128)(2,1)S(1)} %get-tuple-element.77, bf16[192,4096]{1,0:T(8,128)(2,1)S(1)} %copy-done.3), kind=kLoop, calls=%fused_computation.10 | loop fusion | flops 14155776 | bytes 9437184 | tf_op jit(solution)/shard_map/concatenate | solution.py:929
  482.4 71.6 %settle.1 = (f32[1024,768]{1,0:T(8,128)}, bf16[1024,768]{1,0:T(8,128)(2,1)}, bf16[1024,768]{1,0:T(8,128)(2,1)}, bf16[32,32,640]{2,1,0:T(8,128)(2,1)}, f32[32,8,128]{2,1,0:T(8,128)}) custom-call(bf16[576,4096]{1,0:T(8,128)(2,1)} %maximum_maximum_fusion.mix_ref, bf16[4096,768]{1,0:T(8,128)(2,1)} %bitcast.119, bf16[576,768]{1,0:T(8,128)(2,1)} %pad_maximum_fusion.w_ref, ...), custom_call_target="tpu_custom_call" | custom-call | tf_op jit(solution)/shard_map/settle/pallas_call | solution.py:749
  571.3 5.1 add_add_fusion.2
  (172 shorter events, 75.5 us)
Async XLA Ops:
  7.2 209.1 %all-gather.4.cloned.1.call-start = ((), (), s32[]{:S(2)}) async-start(), calls=%async_computation.3 | async-start | bytes 1216512 | tf_op jit(solution)/shard_map/all_gather | solution.py:831
  7.9 216.0 %all-gather.6.cloned.1.call-start = ((), (), s32[]{:S(2)}) async-start(), calls=%async_computation.4 | async-start | bytes 4866048 | tf_op jit(solution)/shard_map/all_gather | solution.py:832
  8.7 230.4 %all-gather.8.cloned.1.call-start = ((), (), s32[]{:S(2)}) async-start(), calls=%async_computation.5 | async-start | bytes 4866048 | tf_op jit(solution)/shard_map/all_gather | solution.py:833
  188.5 27.8 %all-to-all-start = ((bf16[192,4,1024]{2,0,1:T(8,128)(2,1)}), bf16[192,4,1024]{2,0,1:T(8,128)(2,1)S(1)}, u32[]{:S(2)}, u32[]{:S(2)}) async-start(bf16[192,4,1024]{2,0,1:T(8,128)(2,1)} %bitcast.118), calls=%async_computation | async-start | bytes 3145728 | tf_op jit(solution)/shard_map/all_to_all | solution.py:860
  192.1 384.3 %reduce-scatter.2.cloned.1.call-start = ((), (), s32[]{:S(2)}) async-start(), calls=%async_computation.6 | async-start | bytes 10948608 | tf_op jit(solution)/shard_map/reduce_scatter | solution.py:900
  247.9 1.4 copy-start.2
  250.6 2.9 slice-start.4
  250.6 3.4 slice-start.5
  253.2 6.4 %slice-start.2 = ((s8[4718592]{0:T(1024)(128)(4,1)}), s8[4194304]{0:T(1024)(128)(4,1)S(1)}, s32[]{:S(2)}) async-start(s8[4718592]{0:T(1024)(128)(4,1)} %bitcast.145), calls=%async_computation.9 | async-start | bytes 8388608
  254.0 5.6 slice-start.3
  259.6 25.4 %copy-start.6 = (bf16[1024,768]{1,0:T(8,128)(2,1)S(1)}, bf16[1024,768]{1,0:T(8,128)(2,1)}, u32[]{:S(2)}) copy-start(bf16[1024,768]{1,0:T(8,128)(2,1)} %fusion.6) | copy-start | bytes 4718596
  282.3 2.7 copy-start.10
  286.5 3.3 copy-start.11
  289.7 3.0 slice-start
  291.2 1.5 slice-start.1
  302.6 4.0 copy-start
  302.6 2.5 copy-start.5
  314.8 1.3 copy-start.9
  318.6 4.0 copy-start.7
  318.6 24.0 %all-to-all-start.1 = ((bf16[4,192,1024]{2,1,0:T(8,128)(2,1)}), bf16[4,192,1024]{2,1,0:T(8,128)(2,1)S(1)}, u32[]{:S(2)}, u32[]{:S(2)}) async-start(bf16[4,192,1024]{2,1,0:T(8,128)(2,1)} %bitcast.13), calls=%async_computation.1 | async-start | bytes 3145728 | tf_op jit(solution)/shard_map/all_to_all | solution.py:907
  366.9 102.6 %collective-permute-start = (bf16[384,2048]{1,0:T(8,128)(2,1)}, bf16[384,2048]{1,0:T(8,128)(2,1)S(1)}, u32[]{:S(2)}, u32[]{:S(2)}) collective-permute-start(bf16[384,2048]{1,0:T(8,128)(2,1)} %get-tuple-element.43), channel_id=1, source_target_pairs={{0,4},{1,5},{2,6},{3,7},{4,8},{5,9},{6,10},{7,11},{8,12},{9,13},{1... | collective-permute-start | bytes 4718600 | tf_op jit(solution)/shard_map/ppermute | solution.py:917
  371.3 98.3 %collective-permute-start.1 = (bf16[384,2048]{1,0:T(8,128)(2,1)}, bf16[384,2048]{1,0:T(8,128)(2,1)S(1)}, u32[]{:S(2)}, u32[]{:S(2)}) collective-permute-start(bf16[384,2048]{1,0:T(8,128)(2,1)} %get-tuple-element.44), channel_id=1, source_target_pairs={{4,0},{5,1},{6,2},{7,3},{8,4},{9,5},{10,6},{11,7},{12,8},{13,9},{1... | collective-permute-start | bytes 4718600 | tf_op jit(solution)/shard_map/ppermute | solution.py:916
  469.5 4.1 copy-start.3
  554.0 17.3 %copy-start.1 = (f32[1024,768]{1,0:T(8,128)S(1)}, f32[1024,768]{1,0:T(8,128)}, u32[]{:S(2)}) copy-start(f32[1024,768]{1,0:T(8,128)} %copy-done) | copy-start | bytes 9437188
  (2 other events, 1.8 us)
Sparse Core Ops, SparseCore 0:
  10.9 94.9 all-gather.3
  108.8 61.7 all-gather.5
  173.4 65.5 all-gather.7
  314.9 190.9 reduce-scatter.1
where the time goes:
time: 595 us; the launch traced here: 587 us
  Pallas kernels  347 us (58%)
  matrix products  72.3 us (12%)
  local copies, waits for them, and re-layouts  46.7 us (8%)
  waiting for transfers between devices  46.3 us (8%)
  other arithmetic  45.5 us (8%)
  between operations  15 us (3%)
  starting transfers between devices  13.6 us (2%)
    pallas_call x2, Pallas kernels, attend_grad(): pl.pallas_call(functools.partial(grad_kernel, parts, final), grid_spec=pl...  117 us
    pallas_call x1, Pallas kernels, share(): pl.pallas_call(functools.partial(share_kernel, n_dev, rows_w), in_specs=[...  93.1 us
    pallas_call x1, Pallas kernels, settle(): pl.pallas_call(functools.partial(settle_kernel, n_dev, rows_w), in_specs=...  71.6 us
    pallas_call x1, Pallas kernels, attend(): pl.pallas_call(attend_kernel, grid_spec=pltpu.PrefetchScalarGridSpec(num_...  65.1 us
    all_to_all x1, waiting for transfers between devices, body(): lax.all_to_all(ot.reshape(Q_ROWS, GROUP, row_count), 'fsdp', 1, 0, axis_i...  22.7 us
    dot_general x1, matrix products, body(): jnp.einsum('rd,fd->rf', d_ffn, wd_full, preferred_element_type=f32)  22.7 us
    unnamed x48, local copies, waits for them, and re-layouts  19.1 us
    all_to_all x1, waiting for transfers between devices, body(): lax.all_to_all(dctx_t.reshape(GROUP, Q_ROWS, row_count), 'fsdp', 0, 2, ax...  17.6 us
  transfers between devices with their start and end apart: 8, of which 3 were waited for; matrix products, arithmetic and copies ran while one was open for 14% of the time, Pallas kernels for 59%

commit v1 on v0

--- a/solution.py
+++ b/solution.py
@@ -258,8 +258,8 @@
 
 
 def share_kernel(
-    n_dev, rows_w, tok_ref, code_ref, w_ref, x_own, c_out, w_turn, qt_out, kv_out, kvt_out,
-    x_out, w_out, w_wide, w_full, qt_sc, kv_sc, kvt_sc,
+    n_dev, rows_w, tok_ref, code_ref, w_ref, x_own, code_out, ktag_out, w_turn, qt_out, kv_out, kvt_out,
+    c_out, x_out, w_out, w_wide, w_full, qt_sc, kv_sc, kvt_sc,
     w_send, w_recv, c_send, c_recv, part_send, part_recv, mate_send, mate_recv,
     up_send, up_recv, down_send, down_recv, cross_send, cross_recv,
     fwd_send, fwd_recv, keep_sem, x_sem, q_sem, kv_sem, kvt_sem,
@@ -362,7 +362,6 @@
             c_far(j).start()
 
     order = list(range(half, CHUNKS)) + list(range(half))
-    lax.fori_loop(1, n_dev, w_start, 0)
 
     @pl.when((hi == 0) & has_down)
     def _():
@@ -377,6 +376,9 @@
             @pl.when((hi == 1) & has_up)
             def _():
                 up_own(c).start()
+
+        if n == half - 1:
+            lax.fori_loop(1, n_dev, w_start, 0)
 
     for n, c in enumerate(order):
         to_mate(c).wait_recv()
@@ -449,6 +451,36 @@
         for copy in outs(b, inside):
             copy.start()
 
+    keep_c.wait()
+    for j in range(1, GROUP):
+        remote(
+            code_ref, c_out.at[0], c_send.at[j], c_recv.at[2 + lax.rem(s + j, GROUP)], partner
+        ).wait_recv()
+
+    @pl.when(has_down)
+    def _():
+        for b in range(2):
+            remote(code_ref, c_out.at[b], c_send.at[0], c_recv.at[b], partner).wait_recv()
+
+    @pl.when(has_up)
+    def _():
+        for b in range(6, 8):
+            remote(code_ref, c_out.at[b], c_send.at[0], c_recv.at[b], partner).wait_recv()
+
+    for b in range(8):
+        code = c_out[b]
+        if b < 2:
+            code = jnp.where(has_down, code, -2)
+        if b >= 6:
+            code = jnp.where(has_up, code, 2 * n_dev * tok_ref.shape[0])
+        code_out[b] = code
+        tag = jnp.where((code & 1) == 1, (code >> 1) + 1, 0)
+        lanes = tag.shape[1]
+        for r in range(8):
+            turned = jnp.broadcast_to(tag[r : r + 1, :], (lanes, lanes)).T
+            at = (8 * b + r) * lanes
+            ktag_out[at : at + lanes, :] = turned[:, :1]
+
     own_block = 2 + s
     near_block = own_block + 1 - 2 * k
     across_block = mate_block + 1 - 2 * k
@@ -530,31 +562,17 @@
 
     for j in range(1, GROUP):
         c_group(j).wait_send()
-        remote(
-            code_ref, c_out.at[0], c_send.at[j], c_recv.at[2 + lax.rem(s + j, GROUP)], partner
-        ).wait_recv()
 
     @pl.when(sends_far)
     def _():
         for j in range(GROUP):
             c_far(j).wait_send()
-
-    @pl.when(has_down)
-    def _():
-        for b in range(2):
-            remote(code_ref, c_out.at[b], c_send.at[0], c_recv.at[b], partner).wait_recv()
-
-    @pl.when(has_up)
-    def _():
-        for b in range(6, 8):
-            remote(code_ref, c_out.at[b], c_send.at[0], c_recv.at[b], partner).wait_recv()
 
     def w_sent(r, carry):
         w_copy(r).wait_send()
         return carry
 
     lax.fori_loop(1, n_dev, w_sent, 0)
-    keep_c.wait()
     for b in range(2, 6):
         for copy in outs(b, True):
             copy.wait()
@@ -582,16 +600,18 @@
     return pl.pallas_call(
         functools.partial(share_kernel, n_dev, rows_w),
         in_specs=[vmem] * 3,
-        out_specs=[anywhere, anywhere, vmem, anywhere, anywhere, anywhere],
+        out_specs=[anywhere, vmem, vmem, vmem, anywhere, anywhere, anywhere],
         out_shape=[
             jax.ShapeDtypeStruct((GROUP, rows, width), bf16),
             jax.ShapeDtypeStruct((8,) + code.shape, code.dtype),
+            jax.ShapeDtypeStruct((window, 1), code.dtype),
             jax.ShapeDtypeStruct((W_LANES, width), bf16),
             jax.ShapeDtypeStruct((Q_ROWS, own), bf16),
             jax.ShapeDtypeStruct((window, KV_ROWS), bf16),
             jax.ShapeDtypeStruct((KV_ROWS, window), bf16),
         ],
         scratch_shapes=[
+            pltpu.VMEM((8,) + code.shape, code.dtype),
             pltpu.VMEM((8, rows, width), bf16),
             pltpu.VMEM((n_dev,) + w_send.shape[1:], bf16),
             pltpu.VMEM((width, W_LANES), f32),
@@ -616,7 +636,7 @@
 
 
 def settle_kernel(
-    n_dev, rows_w, mix_ref, x_ref, w_ref, vec_ref, own_out, near_out, far_out, w_out, vec_out,
+    n_dev, rows_w, q_ref, kv_ref, x_ref, w_ref, vec_ref, own_out, near_out, far_out, w_out, vec_out,
     wide, slabs, across, near, relay, total,
     w_send, w_recv, vec_send, vec_recv, near_send, near_recv, relay_send, relay_recv,
     far_send, far_recv, keep_sem,
@@ -676,39 +696,26 @@
     keep_vec = pltpu.make_async_copy(vec_ref.at[me], vec_out.at[me], keep_sem.at[1])
     keep_vec.start()
 
-    wide[...] = jnp.zeros_like(wide)
-
-    def add_rows(j, carry):
-        at = pl.ds(pl.multiple_of(j * block, block), block)
-        wide[:MIX_ROWS, :] += mm(mix_ref[:, at], x_ref[at, :])
-        return carry
-
-    lax.fori_loop(0, GROUP, add_rows, 0)
-    turned = wide[...].T.astype(bf16).astype(f32)
-    bias = mm(jnp.ones((8, GROUP * block), bf16), mix_ref[...], NT).astype(bf16)
-    bias_at = slabs.shape[1] - 8
-    for j in range(n_dev):
-        slabs[j, :rows_w, :] = turned[rows_w * j : rows_w * (j + 1), :].astype(bf16)
-        slabs[j, bias_at:, :MIX_ROWS] = bias
-
     def back(t, c):
         at = pl.ds(pl.multiple_of(t * block + c * rows, rows), rows)
-        return mm(mix_ref[:, at], w_ref[...], TN)
+        return mm(q_ref[:, at], w_ref[:Q_ROWS, :], TN) + mm(kv_ref[:, at], w_ref[KV_AT:, :], TN)
+
+    def add_rows(j):
+        at = slice(j * block, (j + 1) * block)
+        wide[:Q_ROWS, :] += mm(q_ref[:, at], x_ref[at, :])
+        wide[Q_ROWS:MIX_ROWS, :] += mm(kv_ref[:, at], x_ref[at, :])
+
+    def w_start(r, carry):
+        w_copy(r).start()
+        return carry
 
     for c in range(PARTS):
         across[c * rows : (c + 1) * rows, :] = back(s_across, c).astype(bf16)
         if c > 0:
             to_relay(c - 1).start()
-
-    def w_start(r, carry):
-        w_copy(r).start()
-        return carry
-
-    lax.fori_loop(1, n_dev, w_start, 0)
-    keep_w = pltpu.make_async_copy(slabs.at[me], w_out.at[me], keep_sem.at[0])
-    keep_w.start()
     mine = back(s_mate, 0)
     to_relay(PARTS - 1).start()
+    wide[...] = jnp.zeros_like(wide)
     for c in range(PARTS):
         to_relay(c).wait_recv()
         other = relay[c * rows : (c + 1) * rows, :].astype(f32)
@@ -716,8 +723,23 @@
         if c + 1 < PARTS:
             mine = back(s_mate, c + 1)
         else:
-            near[:rows, :] = back(s_partner, 0).astype(bf16)
+            add_rows(0)
         to_far(c).start()
+    for j in range(1, GROUP):
+        add_rows(j)
+    turned = wide[...].T
+    one = jnp.ones((8, GROUP * block), bf16)
+    bias_q = mm(one, q_ref[...], NT).astype(bf16)
+    bias_kv = mm(one, kv_ref[...], NT).astype(bf16)
+    bias_at = slabs.shape[1] - 8
+    for j in range(n_dev):
+        slabs[j, :rows_w, :] = turned[rows_w * j : rows_w * (j + 1), :].astype(bf16)
+        slabs[j, bias_at:, :Q_ROWS] = bias_q
+        slabs[j, bias_at:, Q_ROWS:MIX_ROWS] = bias_kv
+    near[:rows, :] = back(s_partner, 0).astype(bf16)
+    lax.fori_loop(1, n_dev, w_start, 0)
+    keep_w = pltpu.make_async_copy(slabs.at[me], w_out.at[me], keep_sem.at[0])
+    keep_w.start()
     for c in range(1, PARTS):
         near[c * rows : (c + 1) * rows, :] = back(s_partner, c).astype(bf16)
         to_near(c - 1).start()
@@ -740,7 +762,7 @@
     keep_vec.wait()
 
 
-def settle(n_dev, rows_w, mix, x, w, vec):
+def settle(n_dev, rows_w, d_q, d_kv, x, w, vec):
     vmem = pl.BlockSpec(memory_space=pltpu.VMEM)
     anywhere = pl.BlockSpec(memory_space=pl.ANY)
     dma = lambda n: pltpu.SemaphoreType.DMA((n,))
@@ -748,7 +770,7 @@
     slabs = (n_dev, rows_w + -rows_w % 8 + 8, W_LANES)
     return pl.pallas_call(
         functools.partial(settle_kernel, n_dev, rows_w),
-        in_specs=[vmem] * 4,
+        in_specs=[vmem] * 5,
         out_specs=[vmem] + [anywhere] * 4,
         out_shape=[
             jax.ShapeDtypeStruct(block, f32),
@@ -769,7 +791,7 @@
             collective_id=1, has_side_effects=True, vmem_limit_bytes=60 << 20
         ),
         name="settle",
-    )(mix, x, w, vec)
+    )(d_q, d_kv, x, w, vec)
 
 
 def body(
@@ -833,21 +855,14 @@
     wd_full = lax.all_gather(w_down, "fsdp", axis=0, tiled=True)
 
     code = (segment_ids * 2 + pad_mask).reshape(8, row_count // 8)
-    x_own, code_win, w_turn, qt, kv, kvt = share(n_dev, rows_w, tokens, code, w_send)
+    x_own, code_win, ktag, w_turn, qt, kv, kvt = share(n_dev, rows_w, tokens, code, w_send)
     x_own = x_own.reshape(own, D)
     code_win = code_win.reshape(window)
-    at = jnp.arange(window)
-    code_win = jnp.where((group_id == 0) & (at < LEN_MAX), -2, code_win)
-    code_win = jnp.where(
-        (group_id == n_group - 1) & (at >= LEN_MAX + own), 2 * n_dev * row_count, code_win
-    )
     code_own = code_win[LEN_MAX : LEN_MAX + own]
-    w_back = jnp.concatenate([w_turn[:Q_ROWS], w_turn[KV_AT:]], axis=0)
     small_all = w_turn[Q_ROWS : Q_ROWS + 10].astype(f32)
     bu_full = small_all[6:].T.reshape(-1)
     bo_full, g1_full, s1_full, bd_full, g2_full, s2_full = [small_all[j] for j in range(6)]
     seg_win = code_win >> 1
-    ktag = jnp.where((code_win & 1) == 1, seg_win + 1, 0).reshape(window, 1)
     seg_own = code_own >> 1
     qtag = (seg_own + 1).reshape(1, own)
     first_seg = seg_own[::BQ]
@@ -878,10 +893,8 @@
     d_hidden = jnp.einsum("rd,fd->rf", d_ffn, wd_full, preferred_element_type=f32)
     d_pre = gelu_back(d_hidden)[0].astype(bf16)
     d_bias_up = jnp.sum(d_pre.astype(f32), axis=0)
-    d_w_up = [
-        jnp.einsum("rd,rf->df", up_in, d_pre[:, D * j : D * (j + 1)], preferred_element_type=f32)
-        for j in range(ff // D)
-    ]
+    d_w_up = jnp.einsum("rd,rf->df", up_in, d_pre, preferred_element_type=f32).astype(bf16)
+    d_w_up = lax.optimization_barrier(d_w_up)
     d_first = d_second + jnp.einsum("rf,df->rd", d_pre, wu_full, preferred_element_type=f32)
     d_mid, d_gain_one, d_shift_one = norm_one_back(d_first)
     d_branch = d_mid.astype(bf16)
@@ -894,7 +907,7 @@
             d_w_down.astype(bf16).reshape(n_dev, -1, D),
             d_w_out.astype(bf16).reshape(n_dev, rows_w, D),
         ]
-        + [v.astype(bf16).reshape(n_dev, rows_w, D) for v in d_w_up],
+        + [d_w_up[:, D * j : D * (j + 1)].reshape(n_dev, rows_w, D) for j in range(n_up)],
         axis=1,
     )
     big_owned = lax.psum_scatter(big_grad, "fsdp", scatter_dimension=0).astype(f32)
@@ -926,7 +939,6 @@
         ],
         axis=1,
     ).astype(bf16)
-    dmix_t = jnp.concatenate([dq_t, dkv], axis=0)
     vecs = jnp.stack([d_bias_out, d_gain_one, d_shift_one, d_bias_down, d_gain_two, d_shift_two])
     vec_send = jnp.concatenate(
         [
@@ -936,7 +948,7 @@
         axis=1,
     )
     vec_send = jnp.pad(vec_send, ((0, 0), (0, 1024 - vec_send.shape[1]))).reshape(n_dev, 8, 128)
-    own_x, near, far, w_got, vec_got = settle(n_dev, rows_w, dmix_t, x_own, w_back, vec_send)
+    own_x, near, far, w_got, vec_got = settle(n_dev, rows_w, dq_t, dkv, x_own, w_turn, vec_send)
     grad_tokens = d_mid + ((own_x + near.astype(f32)) + far.astype(f32))
     got = jnp.sum(w_got.astype(f32).reshape(n_group, GROUP, -1, W_LANES), axis=0)
     got_q = got[:, :, :Q_ROWS].transpose(1, 0, 2).reshape(-1, D)
@@ -945,9 +957,10 @@
     got_k = got_kv[:, :, :, 0].reshape(-1, D)
     got_v = got_kv[:, :, :, 1].reshape(-1, D)
     grad_w_qkv = jnp.concatenate([got_q[:rows_w], got_k[:rows_w], got_v[:rows_w]], axis=1)
-    mine = lambda rows: lax.dynamic_slice(rows[-1], (me * rows_w,), (rows_w,))
+    bias_rows = jnp.stack([got_q[-1], got_v[-1]])
+    bias_own = lax.dynamic_slice(bias_rows, (0, me * rows_w), (2, rows_w))
     vec = jnp.sum(vec_got, axis=0).reshape(-1)[: 10 * rows_w]
-    own_vec = [mine(got_q), mine(got_v)] + [vec[j * rows_w : (j + 1) * rows_w] for j in range(6)]
+    own_vec = [bias_own[0], bias_own[1]] + [vec[j * rows_w : (j + 1) * rows_w] for j in range(6)]
     return (
         layer_out,
         grad_tokens,

time: 595 us -> 587 us (0.987)
  Pallas kernels: 347 us -> 318 us
  waiting for transfers between devices: 46.3 us -> 74.6 us
  other arithmetic: 45.5 us -> 33.9 us
  local copies, waits for them, and re-layouts: 46.7 us -> 40.3 us
    all_gather x1, waiting for transfers between devices: 3.92 us -> 34.1 us  [body(): wd_full = lax.all_gather(w_down, 'fsdp', axis=0, tiled=True)]
    pallas_call x2, Pallas kernels: 117 us -> 99.9 us  [attend_grad(): pl.pallas_call(functools.partial(grad_kernel, parts, final), grid_spec=pl...]
    pallas_call x1, Pallas kernels: 65.1 us -> 50.5 us  [attend(): pl.pallas_call(attend_kernel, grid_spec=pltpu.PrefetchScalarGridSpec(num_...]
    dot_general x4 -> x1, matrix products: 7.45 us -> 16.8 us  [body(): jnp.einsum('rd,rf->df', up_in, d_pre, preferred_element_type=f32)]
    dot_general x1, matrix products: 22.7 us -> 13.8 us  [body(): jnp.einsum('rd,fd->rf', d_ffn, wd_full, preferred_element_type=f32)]
    concatenate x2 -> x1, other arithmetic: 9.66 us -> 1.87 us  [body(): jnp.concatenate([dkv_own[:, :LEN_MAX] + from_left.astype(f32), dkv_own[:,...]
    unnamed x48 -> x36, local copies, waits for them, and re-layouts: 19.1 us -> 17.2 us
  transfers between devices with their start and end apart: 8 -> 8, of which waited for: 3 -> 3; matrix products, arithmetic and copies ran while one was open for 14% -> 12% of each run, Pallas kernels for 59% -> 55%
where the time goes in v1:
time: 587 us; the launch traced here: 576 us
  Pallas kernels  318 us (54%)
  matrix products  75.4 us (13%)
  waiting for transfers between devices  74.6 us (13%)
  local copies, waits for them, and re-layouts  40.3 us (7%)
  other arithmetic  33.9 us (6%)
  starting transfers between devices  19 us (3%)
  between operations  14.8 us (3%)
    pallas_call x2, Pallas kernels, attend_grad(): pl.pallas_call(functools.partial(grad_kernel, parts, final), grid_spec=pl...  99.9 us
    pallas_call x1, Pallas kernels, share(): pl.pallas_call(functools.partial(share_kernel, n_dev, rows_w), in_specs=[...  93.5 us
    pallas_call x1, Pallas kernels, settle(): pl.pallas_call(functools.partial(settle_kernel, n_dev, rows_w), in_specs=...  74.3 us
    pallas_call x1, Pallas kernels, attend(): pl.pallas_call(attend_kernel, grid_spec=pltpu.PrefetchScalarGridSpec(num_...  50.5 us
    all_gather x1, waiting for transfers between devices, body(): wd_full = lax.all_gather(w_down, 'fsdp', axis=0, tiled=True)  34.1 us
    all_to_all x1, waiting for transfers between devices, body(): lax.all_to_all(ot.reshape(Q_ROWS, GROUP, row_count), 'fsdp', 1, 0, axis_i...  19.5 us
    all_to_all x1, waiting for transfers between devices, body(): lax.all_to_all(dctx_t.reshape(GROUP, Q_ROWS, row_count), 'fsdp', 0, 2, ax...  18.9 us
    unnamed x36, local copies, waits for them, and re-layouts  17.2 us
  transfers between devices with their start and end apart: 8, of which 3 were waited for; matrix products, arithmetic and copies ran while one was open for 12% of the time, Pallas kernels for 55%

profile of v1, /device:TPU:0, one launch (start us, length us, event | category | flops | bytes accessed | tf_op | source)
XLA Modules:
  0.0 576.2 jit_solution(17179316686420684035)
XLA Ops:
  16.7 93.5 %share.1 = (bf16[4,1024,768]{2,1,0:T(8,128)(2,1)}, s32[8,8,128]{2,1,0:T(8,128)}, s32[8192,1]{1,0:T(8,128)}, bf16[640,768]{1,0:T(8,128)(2,1)}, bf16[192,4096]{1,0...) custom-call(bf16[1024,768]{1,0:T(8,128)(2,1)} %tok_ref.1, s32[8,128]{1,0:T(8,128)} %add_bitcast_fusion.code_ref, ...), custom_call_target="tpu_custom_call" | custom-call | tf_op jit(solution)/shard_map/share/pallas_call | solution.py:600
  113.5 50.5 %attend.1 = (bf16[192,4096]{1,0:T(8,128)(2,1)}, f32[8,4096]{1,0:T(8,128)}) custom-call(s32[8,2]{1,0:T(8,128)} %copy.127.span, s32[1,4096]{1,0:T(1,128)} %bitcast.135, s32[8192,1]{1,0:T(8,128)} %get-tuple-element.35.ktag_ref, bf16[192,4096]{1,0:T(8,128)(2,1)} %get-tuple-element.36.qt_ref, bf16[8192,384]{1,0:T(8,128)(2,1)} %get-tuple-element.37.kv_ref, ...), custom_call_target="tpu_custom_call" | custom-call | flops 6442450944 | bytes 20971520 | tf_op jit(solution)/shard_map/attend/pallas_call | solution.py:102
  164.0 2.7 copy.147
  166.8 3.6 all-to-all-start
  171.9 19.5 %all-to-all-done = bf16[192,4,1024]{2,0,1:T(8,128)(2,1)S(1)} async-done(((bf16[192,4,1024]{2,0,1:T(8,128)(2,1)}), bf16[192,4,1024]{2,0,1:T(8,128)(2,1)S(1)}, u32[]{:S(2)}, u32[]{:S(2)}) %all-to-all-start) | async-done | bytes 1572896 | tf_op jit(solution)/shard_map/all_to_all | solution.py:875
  192.5 3.9 fusion.22
  196.9 12.7 %multiply_convert_fusion = (bf16[1024,3072]{1,0:T(8,128)(2,1)}, f32[1024,3072]{1,0:T(8,128)}) fusion(f32[3072]{0:T(1024)S(1)} %add.210, bf16[768,3072]{1,0:T(8,128)(2,1)} %all-gather.6.cloned.1.call-done, f32[1024,768]{1,0:T(8,128)S(1)} %get-tuple-element.109, f32[768]{0:T(1024)S(1)} %get-tuple-element.62, f32[768]{0:T(1024)S(1)} %get-tuple-element.63, ...), kind=kOutput, calls=%fused_computation.2 | convolution fusion | flops 4854644736 | bytes 26765312 | tf_op jit(solution)/shard_map/dot_general | solution.py:883
  209.6 34.1 %all-gather.8.cloned.1.call-done = bf16[3072,768]{1,0:T(8,128)(2,1)} async-done(((bf16[96,768]{1,0:T(8,128)(2,1)}), bf16[3072,768]{1,0:T(8,128)(2,1)}) %all-gather.8.cloned.1.call-update) | async-done | bytes 4718608 | tf_op jit(solution)/shard_map/all_gather | solution.py:855
  243.7 8.8 %fusion.23 = (f32[1024]{0:T(1024)S(1)}, f32[1024,768]{1,0:T(8,128)S(1)}) fusion(f32[768]{0:T(1024)S(1)} %get-tuple-element.61, bf16[1024,3072]{1,0:T(8,128)(2,1)} %get-tuple-element.110, bf16[3072,768]{1,0:T(8,128)(2,1)} %all-gather.8.cloned.1.call-done, f32[768]{0:T(1024)S(1)} %get-tuple-element.62, f32[768]{0:T(1024)S(1)} %get-tuple-element.63, ...), kind=kOutput, calls=%fused_computation.139 | convolution fusion | flops 4837342208 | bytes 17323008 | tf_op jit(solution)/shard_map/dot_general | solution.py:886
  258.7 5.5 convolution_convert_fusion.1
  264.2 13.8 %convert_reduce_fusion = (f32[3072]{0:T(1024)S(1)}, bf16[1024,3072]{1,0:T(8,128)(2,1)S(1)}) fusion(bf16[1024,768]{1,0:T(8,128)(2,1)S(1)} %get-tuple-element.70, bf16[3072,768]{1,0:T(8,128)(2,1)S(1)} %bitcast.143, f32[1024,3072]{1,0:T(8,128)} %get-tuple-element.111, f32[3072]{0:T(1024)S(1)} %add.210), kind=kOutput, calls=%fused_computation | convolution fusion | flops 4882166784 | bytes 25190400 | tf_op jit(solution)/shard_map/rd,fd->rf/dot_general | solution.py:893
  280.8 16.8 %convolution_convert_fusion = bf16[768,3072]{1,0:T(8,128)(2,1)S(1)} fusion(bf16[1024,3072]{1,0:T(8,128)(2,1)S(1)} %get-tuple-element.116, f32[1024,768]{1,0:T(8,128)S(1)} %get-tuple-element.109, f32[768]{0:T(1024)S(1)} %get-tuple-element.62, f32[768]{0:T(1024)S(1)} %get-tuple-element.63, f32[1024]{0:T(1024)S(1)} %fusion.10, ...), kind=kOutput, calls=%fused_computation.4 | convolution fusion | flops 4838129664 | bytes 14170112 | tf_op jit(solution)/shard_map/rd,rf->df/dot_general | solution.py:896
  301.6 8.3 %multiply_reduce_fusion = (f32[768]{0:T(1024)S(1)}, f32[1024]{0:T(1024)S(1)}, f32[768]{0:T(1024)S(1)}, f32[1024,768]{1,0:T(8,128)S(1)}) fusion(f32[1024,768]{1,0:T(8,128)S(1)} %get-tuple-element.109, f32[1024]{0:T(1024)S(1)} %fusion.10, f32[1024]{0:T(1024)S(1)} %broadcast_multiply_fusion.1, f32[768]{0:T(1024)S(1)} %get-tuple-element.63, ...), kind=kOutput, calls=%fused_computation.18 | convolution fusion | flops 4839699456 | bytes 20472832 | tf_op jit(solution)/shard_map/rf,df->rd/dot_general | solution.py:898
  309.9 2.8 fusion.16
  321.5 4.3 convolution_convert_fusion.2
  325.8 4.4 all-to-all-start.1
  331.4 18.9 %all-to-all-done.1 = bf16[4,192,1024]{2,1,0:T(8,128)(2,1)} async-done(((bf16[4,192,1024]{2,1,0:T(8,128)(2,1)}), bf16[4,192,1024]{2,1,0:T(8,128)(2,1)}, u32[]{:S(2)}, u32[]{:S(2)}) %all-to-all-start.1) | async-done | bytes 1572896 | tf_op jit(solution)/shard_map/all_to_all | solution.py:920
  350.3 2.7 copy.132
  354.8 24.3 %grad_far.1 = (f32[192,4096]{1,0:T(8,128)}, bf16[384,2048]{1,0:T(8,128)(2,1)}, bf16[384,2048]{1,0:T(8,128)(2,1)}) custom-call(s32[8,2]{1,0:T(8,128)} %copy.134.span, s32[1,4096]{1,0:T(1,128)} %bitcast.136, s32[8192,1]{1,0:T(8,128)} %get-tuple-element.35.ktag_ref, bf16[192,4096]{1,0:T(8,128)(2,1)} %get-tuple-element.36.qt_ref, bf16[192,4096]{1,0:T(8,128)(2,1)} %bitcast.127, ...), custom_call_target="tpu_custom_call" | custom-call | flops 2415919104 | bytes 20971520 | tf_op jit(solution)/shard_map/grad_far/pallas_call | solution.py:209
  379.1 9.4 %collective-permute-start = (bf16[384,2048]{1,0:T(8,128)(2,1)}, bf16[384,2048]{1,0:T(8,128)(2,1)}, u32[]{:S(2)}, u32[]{:S(2)}) collective-permute-start(bf16[384,2048]{1,0:T(8,128)(2,1)} %get-tuple-element.45), channel_id=1, source_target_pairs={{0,4},{1,5},{2,6},{3,7},{4,8},{5,9},{6,10},{7,11},{8,12},{9,13},{1... | collective-permute-start | bytes 4718600 | tf_op jit(solution)/shard_map/ppermute | solution.py:930
  390.8 75.6 %grad_own.1 = (bf16[192,4096]{1,0:T(8,128)(2,1)}, f32[384,4096]{1,0:T(8,128)}) custom-call(s32[8,2]{1,0:T(8,128)} %copy.134.span, s32[1,4096]{1,0:T(1,128)} %bitcast.137, s32[8192,1]{1,0:T(8,128)} %get-tuple-element.35.ktag_ref, bf16[192,4096]{1,0:T(8,128)(2,1)} %get-tuple-element.36.qt_ref, bf16[192,4096]{1,0:T(8,128)(2,1)} %bitcast.128, ...), custom_call_target="tpu_custom_call" | custom-call | flops 12079595520 | bytes 20971520 | tf_op jit(solution)/shard_map/grad_own/pallas_call | solution.py:209
  466.4 4.8 add_convert_fusion.2
  473.1 74.3 %settle.1 = (f32[1024,768]{1,0:T(8,128)}, bf16[1024,768]{1,0:T(8,128)(2,1)}, bf16[1024,768]{1,0:T(8,128)(2,1)}, bf16[32,32,640]{2,1,0:T(8,128)(2,1)}, f32[32,8,128]{2,1,0:T(8,128)}) custom-call(bf16[192,4096]{1,0:T(8,128)(2,1)} %get-tuple-element.43.q_ref, bf16[384,4096]{1,0:T(8,128)(2,1)} %pad_maximum_fusion.kv_ref, bf16[4096,768]{1,0:T(8,128)(2,1)} %bitcast.117, ...), custom_call_target="tpu_custom_call" | custom-call | tf_op jit(solution)/shard_map/settle/pallas_call | solution.py:771
  561.0 5.1 add_add_fusion.2
  (154 shorter events, 61.1 us)
Async XLA Ops:
  7.2 184.2 %all-gather.4.cloned.1.call-start = ((), (), s32[]{:S(2)}) async-start(), calls=%async_computation.3 | async-start | bytes 1216512 | tf_op jit(solution)/shard_map/all_gather | solution.py:853
  7.9 189.0 %all-gather.6.cloned.1.call-start = ((), (), s32[]{:S(2)}) async-start(), calls=%async_computation.4 | async-start | bytes 4866048 | tf_op jit(solution)/shard_map/all_gather | solution.py:854
  8.7 235.0 %all-gather.8.cloned.1.call-start = ((), (), s32[]{:S(2)}) async-start(), calls=%async_computation.5 | async-start | bytes 4866048 | tf_op jit(solution)/shard_map/all_gather | solution.py:855
  166.8 24.6 %all-to-all-start = ((bf16[192,4,1024]{2,0,1:T(8,128)(2,1)}), bf16[192,4,1024]{2,0,1:T(8,128)(2,1)S(1)}, u32[]{:S(2)}, u32[]{:S(2)}) async-start(bf16[192,4,1024]{2,0,1:T(8,128)(2,1)} %bitcast.116), calls=%async_computation | async-start | bytes 3145728 | tf_op jit(solution)/shard_map/all_to_all | solution.py:875
  170.3 395.8 %reduce-scatter.2.cloned.1.call-start = ((), (), s32[]{:S(2)}) async-start(), calls=%async_computation.6 | async-start | bytes 10948608 | tf_op jit(solution)/shard_map/reduce_scatter | solution.py:913
  191.4 1.1 copy-start.2
  196.4 104.2 %copy-start = (f32[1024,768]{1,0:T(8,128)}, f32[1024,768]{1,0:T(8,128)S(1)}, u32[]{:S(2)}) copy-start(f32[1024,768]{1,0:T(8,128)S(1)} %get-tuple-element.109) | copy-start | bytes 9437188
  252.5 1.4 copy-start.1
  255.2 2.9 slice-start.4
  255.2 3.4 slice-start.5
  257.8 6.4 %slice-start.2 = ((s8[4718592]{0:T(1024)(128)(4,1)}), s8[4194304]{0:T(1024)(128)(4,1)S(1)}, s32[]{:S(2)}) async-start(s8[4718592]{0:T(1024)(128)(4,1)} %bitcast.142), calls=%async_computation.9 | async-start | bytes 8388608
  258.7 5.6 slice-start.3
  278.1 2.7 copy-start.5
  297.5 3.7 slice-start
  297.9 3.8 slice-start.1
  312.8 1.6 copy-start.3
  313.1 2.7 copy-start.4
  325.8 24.5 %all-to-all-start.1 = ((bf16[4,192,1024]{2,1,0:T(8,128)(2,1)}), bf16[4,192,1024]{2,1,0:T(8,128)(2,1)}, u32[]{:S(2)}, u32[]{:S(2)}) async-start(bf16[4,192,1024]{2,1,0:T(8,128)(2,1)} %bitcast.129), calls=%async_computation.1 | async-start | bytes 3145728 | tf_op jit(solution)/shard_map/all_to_all | solution.py:920
  379.1 87.4 %collective-permute-start = (bf16[384,2048]{1,0:T(8,128)(2,1)}, bf16[384,2048]{1,0:T(8,128)(2,1)}, u32[]{:S(2)}, u32[]{:S(2)}) collective-permute-start(bf16[384,2048]{1,0:T(8,128)(2,1)} %get-tuple-element.45), channel_id=1, source_target_pairs={{0,4},{1,5},{2,6},{3,7},{4,8},{5,9},{6,10},{7,11},{8,12},{9,13},{1... | collective-permute-start | bytes 4718600 | tf_op jit(solution)/shard_map/ppermute | solution.py:930
  388.4 78.0 %collective-permute-start.1 = (bf16[384,2048]{1,0:T(8,128)(2,1)}, bf16[384,2048]{1,0:T(8,128)(2,1)}, u32[]{:S(2)}, u32[]{:S(2)}) collective-permute-start(bf16[384,2048]{1,0:T(8,128)(2,1)} %get-tuple-element.46), channel_id=1, source_target_pairs={{4,0},{5,1},{6,2},{7,3},{8,4},{9,5},{10,6},{11,7},{12,8},{13,9},{1... | collective-permute-start | bytes 4718600 | tf_op jit(solution)/shard_map/ppermute | solution.py:929
Sparse Core Ops, SparseCore 0:
  10.9 99.8 all-gather.3
  113.7 63.0 all-gather.5
  179.7 63.9 all-gather.7
  321.6 197.6 reduce-scatter.1

commit v2 on v1

--- a/solution.py
+++ b/solution.py
@@ -794,6 +794,62 @@
     )(d_q, d_kv, x, w, vec)
 
 
+def swap_kernel(spread, in_ref, out_ref, send, recv, keep_sem):
+    me = lax.axis_index("fsdp")
+    s = me % GROUP
+    start = me - s
+    width = (in_ref if spread else out_ref).shape[1] // GROUP
+
+    barrier = pltpu.get_barrier_semaphore()
+    for j in range(1, GROUP):
+        target = start + lax.rem(s + j, GROUP)
+        pl.semaphore_signal(barrier, inc=1, device_id=(target,), device_id_type=MESH)
+    pl.semaphore_wait(barrier, GROUP - 1)
+
+    def cols(ref, t):
+        return ref.at[:, pl.ds(pl.multiple_of(t * width, width), width)]
+
+    def rows(ref, t):
+        return ref.at[pl.ds(pl.multiple_of(t * Q_ROWS, Q_ROWS), Q_ROWS)]
+
+    def ends(t):
+        if spread:
+            return cols(in_ref, t), rows(out_ref, s)
+        return rows(in_ref, t), cols(out_ref, s)
+
+    def copy(j):
+        t = lax.rem(s + j, GROUP)
+        src, dst = ends(t)
+        return remote(src, dst, send.at[j], recv.at[j], start + t)
+
+    for j in (2, 1, 3):
+        copy(j).start()
+    src, dst = ends(s)
+    keep = pltpu.make_async_copy(src, dst, keep_sem.at[0])
+    keep.start()
+    for j in range(1, GROUP):
+        copy(j).wait()
+    keep.wait()
+
+
+def swap(x, spread):
+    shape = (x.shape[0] * GROUP, x.shape[1] // GROUP) if spread else (
+        x.shape[0] // GROUP, x.shape[1] * GROUP
+    )
+    dma = lambda n: pltpu.SemaphoreType.DMA((n,))
+    return pl.pallas_call(
+        functools.partial(swap_kernel, spread),
+        in_specs=[pl.BlockSpec(memory_space=pltpu.VMEM)],
+        out_specs=pl.BlockSpec(memory_space=pltpu.VMEM),
+        out_shape=jax.ShapeDtypeStruct(shape, x.dtype),
+        scratch_shapes=[dma(GROUP), dma(GROUP), dma(1)],
+        compiler_params=pltpu.CompilerParams(
+            collective_id=2 if spread else 3, has_side_effects=True
+        ),
+        name="swap_out" if spread else "swap_back",
+    )(x)
+
+
 def body(
     n_dev,
     tokens,
@@ -824,7 +880,6 @@
     n_group = n_dev // GROUP
     up = [(i, i + GROUP) for i in range(n_dev - GROUP)]
     down = [(i + GROUP, i) for i in range(n_dev - GROUP)]
-    groups = [[GROUP * g + j for j in range(GROUP)] for g in range(n_group)]
 
     wq = w_qkv[:, :D].reshape(rows_w, GROUP, Q_ROWS)
     wk = w_qkv[:, D : 2 * D].reshape(rows_w, GROUP, OWN_HEADS, 1, HEAD_DIM)
@@ -850,9 +905,11 @@
     bias_cut = jnp.pad(bias_cut.astype(bf16)[:, None], ((0, 0), (fill, 7), (0, 0)))
     w_send = jnp.concatenate([w_cut, bias_cut], axis=1)
     ff = w_up.shape[1]
-    wo_full = lax.all_gather(w_out, "fsdp", axis=0, tiled=True)
+    out_down = jnp.concatenate([w_out, w_down], axis=0)
+    out_down = lax.all_gather(out_down, "fsdp", axis=0)
+    wo_full = out_down[:, :rows_w].reshape(D, D)
+    wd_full = lax.optimization_barrier(out_down[:, rows_w:].reshape(ff, D))
     wu_full = lax.all_gather(w_up, "fsdp", axis=0, tiled=True)
-    wd_full = lax.all_gather(w_down, "fsdp", axis=0, tiled=True)
 
     code = (segment_ids * 2 + pad_mask).reshape(8, row_count // 8)
     x_own, code_win, ktag, w_turn, qt, kv, kvt = share(n_dev, rows_w, tokens, code, w_send)
@@ -872,14 +929,12 @@
     spans = [jnp.stack([low // b, (high + b - 1) // b], axis=1) for b in (FK, BK)]
 
     ot, lse = attend(spans[0], qtag, ktag, qt, kv, kvt)
-    ctx_t = lax.all_to_all(
-        ot.reshape(Q_ROWS, GROUP, row_count), "fsdp", 1, 0, axis_index_groups=groups, tiled=True
-    ).reshape(D, row_count)
+    ctx_t = swap(ot, True)
 
     tokens_f = tokens.astype(f32)
     branch = jnp.einsum("ir,io->ro", ctx_t, wo_full, preferred_element_type=f32) + bo_full
     first, norm_one_back = jax.vjp(norm_rows, tokens_f + branch, g1_full, s1_full)
-    up_in = first.astype(bf16)
+    up_in = lax.optimization_barrier(first.astype(bf16))
     pre_act = jnp.dot(up_in, wu_full, preferred_element_type=f32) + bu_full
     gelu_val, gelu_back = jax.vjp(gelu_exact, pre_act)
     hidden = gelu_val.astype(bf16)
@@ -917,9 +972,7 @@
         [big_owned[rows_d + rows_w * (j + 1) : rows_d + rows_w * (j + 2)] for j in range(n_up)], axis=1
     )
 
-    d_out = lax.all_to_all(
-        dctx_t.reshape(GROUP, Q_ROWS, row_count), "fsdp", 0, 2, axis_index_groups=groups, tiled=True
-    ).reshape(Q_ROWS, own)
+    d_out = swap(dctx_t, False)
     edge, inside = LEN_MAX // BK, own // BK
     far_parts = ((0, edge), (edge + inside, 2 * edge + inside))
     own_parts = ((edge, edge + inside),)

time: 587 us -> 570 us (0.971)
  waiting for transfers between devices: 74.6 us -> 1.44 us
  Pallas kernels: 318 us -> 389 us
  matrix products: 75.4 us -> 59 us
    pallas_call x0 -> x2, Pallas kernels: none -> 43.8 us  [swap(): pl.pallas_call(functools.partial(swap_kernel, spread), in_specs=[pl.Block...]
    all_to_all x2 -> x0, waiting for transfers between devices: 38.4 us -> none  [the longest x1 19.5 us: body(): lax.all_to_all(ot.reshape(Q_ROWS, GROUP, row_count), 'fsdp', 1, 0, axis_i...]
    all_gather x2 -> x1, waiting for transfers between devices: 34.1 us -> 0.02 us  [body(): out_down = lax.all_gather(out_down, 'fsdp', axis=0)]
    dot_general x1, matrix products: 16.8 us -> 5.56 us  [body(): jnp.einsum('rd,rf->df', up_in, d_pre, preferred_element_type=f32)]
    pallas_call x1, Pallas kernels: 93.5 us -> 104 us  [share(): pl.pallas_call(functools.partial(share_kernel, n_dev, rows_w), in_specs=[...]
    ppermute x1, starting transfers between devices: 9.38 us -> 17.9 us  [body(): from_left = lax.ppermute(dkv_right, 'fsdp', up)]
    all_to_all x2 -> x0, starting transfers between devices: 7.96 us -> none  [the longest x1 4.39 us: body(): lax.all_to_all(dctx_t.reshape(GROUP, Q_ROWS, row_count), 'fsdp', 0, 2, ax...]
    pallas_call x1, Pallas kernels: 50.5 us -> 58.4 us  [attend(): pl.pallas_call(attend_kernel, grid_spec=pltpu.PrefetchScalarGridSpec(num_...]
  transfers between devices with their start and end apart: 8 -> 5, of which waited for: 3 -> 1; matrix products, arithmetic and copies ran while one was open for 12% -> 10% of each run, Pallas kernels for 55% -> 69%
where the time goes in v2:
time: 570 us; the launch traced here: 561 us
  Pallas kernels  389 us (68%)
  matrix products  59 us (10%)
  local copies, waits for them, and re-layouts  42.1 us (7%)
  other arithmetic  35.2 us (6%)
  starting transfers between devices  19.6 us (3%)
  between operations  14.8 us (3%)
    pallas_call x2, Pallas kernels, attend_grad(): pl.pallas_call(functools.partial(grad_kernel, parts, final), grid_spec=pl...  105 us
    pallas_call x1, Pallas kernels, share(): pl.pallas_call(functools.partial(share_kernel, n_dev, rows_w), in_specs=[...  104 us
    pallas_call x1, Pallas kernels, settle(): pl.pallas_call(functools.partial(settle_kernel, n_dev, rows_w), in_specs=...  77.4 us
    pallas_call x1, Pallas kernels, attend(): pl.pallas_call(attend_kernel, grid_spec=pltpu.PrefetchScalarGridSpec(num_...  58.4 us
    pallas_call x2, Pallas kernels, swap(): pl.pallas_call(functools.partial(swap_kernel, spread), in_specs=[pl.Block...  43.8 us
    ppermute x1, starting transfers between devices, body(): from_left = lax.ppermute(dkv_right, 'fsdp', up)  17.9 us
    dot_general x1, matrix products, body(): jnp.einsum('rd,fd->rf', d_ffn, wd_full, preferred_element_type=f32)  13.9 us
    unnamed x37, local copies, waits for them, and re-layouts  13.9 us
  transfers between devices with their start and end apart: 5, of which 1 were waited for; matrix products, arithmetic and copies ran while one was open for 10% of the time, Pallas kernels for 69%

profile of v2, /device:TPU:0, one launch (start us, length us, event | category | flops | bytes accessed | tf_op | source)
XLA Modules:
  0.0 560.6 jit_solution(8074125640236923225)
XLA Ops:
  17.0 103.6 %share.1 = (bf16[4,1024,768]{2,1,0:T(8,128)(2,1)}, s32[8,8,128]{2,1,0:T(8,128)}, s32[8192,1]{1,0:T(8,128)}, bf16[640,768]{1,0:T(8,128)(2,1)}, bf16[192,4096]{1,0...) custom-call(bf16[1024,768]{1,0:T(8,128)(2,1)} %tok_ref.1, s32[8,128]{1,0:T(8,128)} %add_bitcast_fusion.code_ref, ...), custom_call_target="tpu_custom_call" | custom-call | tf_op jit(solution)/shard_map/share/pallas_call | solution.py:600
  125.0 58.4 %attend.1 = (bf16[192,4096]{1,0:T(8,128)(2,1)}, f32[8,4096]{1,0:T(8,128)}) custom-call(s32[8,2]{1,0:T(8,128)} %copy.120.span, s32[1,4096]{1,0:T(1,128)} %bitcast.123, s32[8192,1]{1,0:T(8,128)} %get-tuple-element.35.ktag_ref, bf16[192,4096]{1,0:T(8,128)(2,1)} %get-tuple-element.36.qt_ref, bf16[8192,384]{1,0:T(8,128)(2,1)} %get-tuple-element.37.kv_ref, ...), custom_call_target="tpu_custom_call" | custom-call | flops 6442450944 | bytes 20971520 | tf_op jit(solution)/shard_map/attend/pallas_call | solution.py:102
  183.5 21.9 %swap_out.1 = bf16[768,1024]{1,0:T(8,128)(2,1)} custom-call(bf16[192,4096]{1,0:T(8,128)(2,1)} %get-tuple-element.39.in_ref.ot_ref), custom_call_target="tpu_custom_call" | custom-call | tf_op jit(solution)/shard_map/swap_out/pallas_call | solution.py:840
  206.9 5.3 slice.239
  216.0 10.9 %multiply_convert_fusion = (bf16[1024,3072]{1,0:T(8,128)(2,1)S(1)}, f32[1024,3072]{1,0:T(8,128)}) fusion(f32[3072]{0:T(1024)S(1)} %add.210, bf16[1024,768]{1,0:T(8,128)(2,1)} %fusion.4, bf16[768,3072]{1,0:T(8,128)(2,1)} %all-gather.4.cloned.1.call-done), kind=kOutput, calls=%fused_computation.2 | convolution fusion | flops 4850712576 | bytes 25178112 | tf_op jit(solution)/shard_map/dot_general | solution.py:938
  227.0 7.7 %fusion.20 = (f32[1024]{0:T(1024)S(1)}, f32[1024,768]{1,0:T(8,128)S(1)}) fusion(f32[768]{0:T(1024)S(1)} %get-tuple-element.61, bf16[1024,3072]{1,0:T(8,128)(2,1)S(1)} %get-tuple-element.110, bf16[3072,768]{1,0:T(8,128)(2,1)} %bitcast.111, f32[768]{0:T(1024)S(1)} %get-tuple-element.62, f32[768]{0:T(1024)S(1)} %get-tuple-element.63, f32[1024]{0:T(1024)S(1)} %fusion.10, ...), kind=kOutput, calls=%fused_computation.138 | convolution fusion | flops 4837342208 | bytes 17323008 | tf_op jit(solution)/shard_map/dot_general | solution.py:941
  237.4 2.6 fusion.14
  240.4 5.6 %convolution_convert_fusion.1 = bf16[3072,768]{1,0:T(8,128)(2,1)S(1)} fusion(bf16[1024,3072]{1,0:T(8,128)(2,1)S(1)} %get-tuple-element.110, bf16[1024,768]{1,0:T(8,128)(2,1)S(1)} %get-tuple-element.70), kind=kOutput, calls=%fused_computation.5 | convolution fusion | flops 4834197504 | bytes 12582912 | tf_op jit(solution)/shard_map/rf,rd->fd/dot_general | solution.py:947
  246.0 13.9 %convert_reduce_fusion = (f32[3072]{0:T(1024)S(1)}, bf16[1024,3072]{1,0:T(8,128)(2,1)S(1)}) fusion(bf16[1024,768]{1,0:T(8,128)(2,1)S(1)} %get-tuple-element.70, bf16[3072,768]{1,0:T(8,128)(2,1)S(1)} %bitcast.114, f32[1024,3072]{1,0:T(8,128)} %get-tuple-element.111, f32[3072]{0:T(1024)S(1)} %add.210), kind=kOutput, calls=%fused_computation | convolution fusion | flops 4882166784 | bytes 25190400 | tf_op jit(solution)/shard_map/rd,fd->rf/dot_general | solution.py:948
  260.0 2.7 copy-done.10
  262.6 5.6 convolution_convert_fusion
  268.2 9.6 %multiply_reduce_fusion = (f32[768]{0:T(1024)S(1)}, f32[1024]{0:T(1024)S(1)}, f32[768]{0:T(1024)S(1)}, f32[1024,768]{1,0:T(8,128)S(1)}) fusion(f32[1024,768]{1,0:T(8,128)S(1)} %get-tuple-element.109, f32[1024]{0:T(1024)S(1)} %fusion.10, f32[1024]{0:T(1024)S(1)} %broadcast_multiply_fusion.1, f32[768]{0:T(1024)S(1)} %get-tuple-element.63, ...), kind=kOutput, calls=%fused_computation.18 | convolution fusion | flops 4839699456 | bytes 20472832 | tf_op jit(solution)/shard_map/rf,df->rd/dot_general | solution.py:953
  279.3 2.8 constant_dynamic-update-slice_fusion.11
  292.2 2.6 convolution_convert_fusion.2.in_ref
  294.7 21.9 %swap_back.1.dot_ref = bf16[192,4096]{1,0:T(8,128)(2,1)} custom-call(bf16[768,1024]{1,0:T(8,128)(2,1)} %convolution_convert_fusion.2.in_ref), custom_call_target="tpu_custom_call" | custom-call | tf_op jit(solution)/shard_map/swap_back/pallas_call | solution.py:840
  316.6 22.0 %grad_far.1 = (f32[192,4096]{1,0:T(8,128)}, bf16[384,2048]{1,0:T(8,128)(2,1)}, bf16[384,2048]{1,0:T(8,128)(2,1)}) custom-call(s32[8,2]{1,0:T(8,128)} %copy.125.span, s32[1,4096]{1,0:T(1,128)} %bitcast.124, s32[8192,1]{1,0:T(8,128)} %get-tuple-element.35.ktag_ref, bf16[192,4096]{1,0:T(8,128)(2,1)} %get-tuple-element.36.qt_ref, ...), custom_call_target="tpu_custom_call" | custom-call | flops 2415919104 | bytes 20971520 | tf_op jit(solution)/shard_map/grad_far/pallas_call | solution.py:209
  338.7 17.9 %collective-permute-start = (bf16[384,2048]{1,0:T(8,128)(2,1)}, bf16[384,2048]{1,0:T(8,128)(2,1)S(1)}, u32[]{:S(2)}, u32[]{:S(2)}) collective-permute-start(bf16[384,2048]{1,0:T(8,128)(2,1)} %get-tuple-element.45), channel_id=1, source_target_pairs={{0,4},{1,5},{2,6},{3,7},{4,8},{5,9},{6,10},{7,11},{8,12},{9,13},{1... | collective-permute-start | bytes 4718600 | tf_op jit(solution)/shard_map/ppermute | solution.py:983
  359.7 83.3 %grad_own.1 = (bf16[192,4096]{1,0:T(8,128)(2,1)}, f32[384,4096]{1,0:T(8,128)}) custom-call(s32[8,2]{1,0:T(8,128)} %copy.125.span, s32[1,4096]{1,0:T(1,128)} %bitcast.125, s32[8192,1]{1,0:T(8,128)} %get-tuple-element.35.ktag_ref, bf16[192,4096]{1,0:T(8,128)(2,1)} %get-tuple-element.36.qt_ref, bf16[192,4096]{1,0:T(8,128)(2,1)} %swap_back.1.dot_ref, ...), custom_call_target="tpu_custom_call" | custom-call | flops 12079595520 | bytes 20971520 | tf_op jit(solution)/shard_map/grad_own/pallas_call | solution.py:209
  443.7 4.0 add_convert_fusion.2
  447.7 1.9 pad_maximum_fusion.kv_ref
  449.6 77.4 %settle.1 = (f32[1024,768]{1,0:T(8,128)}, bf16[1024,768]{1,0:T(8,128)(2,1)}, bf16[1024,768]{1,0:T(8,128)(2,1)}, bf16[32,32,640]{2,1,0:T(8,128)(2,1)}, f32[32,8,128]{2,1,0:T(8,128)}) custom-call(bf16[192,4096]{1,0:T(8,128)(2,1)} %get-tuple-element.43.q_ref, bf16[384,4096]{1,0:T(8,128)(2,1)} %pad_maximum_fusion.kv_ref, bf16[4096,768]{1,0:T(8,128)(2,1)} %bitcast.104, ...), custom_call_target="tpu_custom_call" | custom-call | tf_op jit(solution)/shard_map/settle/pallas_call | solution.py:771
  529.4 1.9 reshape.509
  531.4 2.0 fusion.16
  545.4 5.1 add_add_fusion.2
  (150 shorter events, 55.2 us)
Async XLA Ops:
  7.2 198.3 %all-gather.6.cloned.1.call-start = ((), (), s32[]{:S(2)}) async-start(), calls=%async_computation.3 | async-start | bytes 6082560 | tf_op jit(solution)/shard_map/all_gather | solution.py:909
  8.8 207.2 %all-gather.4.cloned.1.call-start = ((), (), s32[]{:S(2)}) async-start(), calls=%async_computation.1 | async-start | bytes 4866048 | tf_op jit(solution)/shard_map/all_gather | solution.py:912
  9.6 540.9 %reduce-scatter.2.cloned.1.call-start = ((), (), s32[]{:S(2)}) async-start(), calls=%async_computation.2 | async-start | bytes 10948608 | tf_op jit(solution)/shard_map/reduce_scatter | solution.py:968
  206.8 5.3 copy-start.7
  206.8 5.3 copy-start.3
  206.8 5.3 copy-start.5
  234.7 1.4 copy-start.2
  240.0 6.0 %slice-start = ((s8[4718592]{0:T(1024)(128)(4,1)}), s8[4194304]{0:T(1024)(128)(4,1)S(1)}, s32[]{:S(2)}) async-start(s8[4718592]{0:T(1024)(128)(4,1)} %bitcast.112), calls=%async_computation.4 | async-start | bytes 8388608
  240.4 5.6 %slice-start.1 = ((s8[4718592]{0:T(1024)(128)(4,1)}), s8[524288]{0:T(1024)(128)(4,1)S(1)}, s32[]{:S(2)}) async-start(s8[4718592]{0:T(1024)(128)(4,1)} %bitcast.112), calls=%async_computation.5 | async-start | bytes 1048576
  246.0 16.6 %copy-start.6 = (bf16[1024,768]{1,0:T(8,128)(2,1)S(1)}, bf16[1024,768]{1,0:T(8,128)(2,1)}, u32[]{:S(2)}) copy-start(bf16[1024,768]{1,0:T(8,128)(2,1)} %fusion.4) | copy-start | bytes 4718596
  260.0 2.7 copy-start.10
  279.3 3.2 copy-start
  282.1 1.4 copy-start.4
  290.9 1.3 copy-start.8
  338.7 105.0 %collective-permute-start = (bf16[384,2048]{1,0:T(8,128)(2,1)}, bf16[384,2048]{1,0:T(8,128)(2,1)S(1)}, u32[]{:S(2)}, u32[]{:S(2)}) collective-permute-start(bf16[384,2048]{1,0:T(8,128)(2,1)} %get-tuple-element.45), channel_id=1, source_target_pairs={{0,4},{1,5},{2,6},{3,7},{4,8},{5,9},{6,10},{7,11},{8,12},{9,13},{1... | collective-permute-start | bytes 4718600 | tf_op jit(solution)/shard_map/ppermute | solution.py:983
  356.6 87.1 %collective-permute-start.1 = (bf16[384,2048]{1,0:T(8,128)(2,1)}, bf16[384,2048]{1,0:T(8,128)(2,1)S(1)}, u32[]{:S(2)}, u32[]{:S(2)}) collective-permute-start(bf16[384,2048]{1,0:T(8,128)(2,1)} %get-tuple-element.46), channel_id=1, source_target_pairs={{4,0},{5,1},{6,2},{7,3},{8,4},{9,5},{10,6},{11,7},{12,8},{13,9},{1... | collective-permute-start | bytes 4718600 | tf_op jit(solution)/shard_map/ppermute | solution.py:982
  527.0 18.4 %copy-start.1 = (f32[1024,768]{1,0:T(8,128)S(1)}, f32[1024,768]{1,0:T(8,128)}, u32[]{:S(2)}) copy-start(f32[1024,768]{1,0:T(8,128)} %copy-done) | copy-start | bytes 9437188
  538.5 0.7 copy-start.9
Sparse Core Ops, SparseCore 0:
  11.5 111.0 all-gather.5
  125.4 64.9 all-gather.3
  291.0 217.8 reduce-scatter.1
